TPU v7x, 128 devices: a whole 4x4x4 slice. The times are simulated.
128 devices in a mesh: tm: 8 (over y, x_lo), inp: 16 (over z, x_hi, core).
Axes of the slice: x: 4 (x_hi: 2, x_lo: 2; x = x_hi * 2 + x_lo), y: 4, z: 4, core: 2. Of those that a mesh axis runs over, the one named last changes fastest.
Arguments:
- voltages: bfloat16 [1024, 1048576], P('inp', 'tm'), may hold values from -6 to 6
- coefficients: float32 [16, 8192], replicated, may hold values from -1.5 to 1.5
Outputs:
- visibilities: float32 [2, 128, 1024, 1024], P(None, ('tm', 'inp'))
All inputs are finite; a program needn't handle non-finite values.
Results may differ from a plain program's by a relative error of at most 0.0003.
Values may be sent and summed in bfloat16 or wider, within the bound.
No kernel may reach another device: no remote copies, remote signals or barrier semaphores. Data moves between devices by JAX's collectives and lax.ppermute only.
A program may use at most 192 MiB of HBM per device.

v0:
```python
import functools

import jax
import jax.numpy as jnp
import numpy as np
from jax import lax
from jax.experimental import pallas as pl
from jax.experimental.pallas import tpu as pltpu
from jax.sharding import PartitionSpec as P

NFFT = 8192
TAPS = 16
CH = 128
CH0 = 1024
LANES = 128
CHUNK = 256
ROWS = 16
F32 = jnp.float32
BF16 = jnp.bfloat16


def twiddles():
    channel = CH0 + np.arange(CH)
    small = 2.0 * np.pi / NFFT * (np.arange(CHUNK)[:, None] * channel[None, :] % NFFT)
    base = 2.0 * np.pi / NFFT * (np.arange(NFFT // CHUNK)[:, None] * CHUNK * channel[None, :] % NFFT)
    small = np.stack([np.cos(small), -np.sin(small)]) * NFFT ** (-0.5)
    base = np.stack([np.cos(base), -np.sin(base)], axis=1)
    return jnp.asarray(small, F32), jnp.asarray(base, F32)


def split(value):
    high = value.astype(BF16)
    return high, (value - high.astype(F32)).astype(BF16)


def terms(carried, frames):
    if carried:
        return [[(t, frames + s - t) for t in range(s + 1, TAPS)] for s in range(TAPS - 1)]
    return [[(t, s - t) for t in range(min(s, TAPS - 1) + 1)] for s in range(frames)]


def channelize(carried, frames, inputs, *refs):
    x_refs, (h_ref, small_ref, base_ref, out_ref) = refs[:frames], refs[frames : frames + 4]
    slots, acc_ref = (refs[frames + 4 : frames + 8], refs[frames + 8 : frames + 12]), refs[frames + 12]
    plan = terms(carried, frames)
    step = pl.program_id(0)

    @pl.when(step == 0)
    def _():
        acc_ref[...] = jnp.zeros_like(acc_ref)
        for ref in slots[1]:
            ref[...] = jnp.zeros_like(ref)

    def fill(part):
        high_ref, low_ref, table_high_ref, table_low_ref = slots[part]
        base = base_ref[2 * step + part]
        real, imag = small_ref[0], small_ref[1]
        turn_real, turn_imag = base[0:1], base[1:2]
        table = (real * turn_real - imag * turn_imag, real * turn_imag + imag * turn_real)
        for half in range(2):
            high, low = split(table[half])
            table_high_ref[:, half * CH : (half + 1) * CH] = high
            table_low_ref[:, half * CH : (half + 1) * CH] = low
        for block in range(CHUNK // LANES):
            here = slice(block * LANES, (block + 1) * LANES)
            lanes = slice(part * CHUNK + block * LANES, part * CHUNK + (block + 1) * LANES)
            taps = [jnp.broadcast_to(h_ref[t : t + 1, lanes], (ROWS, LANES)) for t in range(TAPS)]
            for row in range(0, inputs, ROWS):
                x = [ref[row : row + ROWS, lanes].astype(F32) for ref in x_refs]
                for s, products in enumerate(plan):
                    value = None
                    for t, frame in products:
                        product = taps[t] * x[frame]
                        value = product if value is None else value + product
                    high, low = split(value)
                    at = slice(s * inputs + row, s * inputs + row + ROWS)
                    high_ref[at, here] = high
                    low_ref[at, here] = low

    def contract(part):
        high_ref, low_ref, table_high_ref, table_low_ref = slots[part]
        dot = functools.partial(jnp.dot, preferred_element_type=F32)
        high = high_ref[...]
        table_high = table_high_ref[...]
        acc_ref[...] += dot(high, table_high) + dot(high, table_low_ref[...]) + dot(low_ref[...], table_high)

    fill(0)
    contract(1)
    fill(1)
    contract(0)

    @pl.when(step == pl.num_programs(0) - 1)
    def _():
        contract(1)
        for s in range(len(plan)):
            rows = slice(s * inputs, (s + 1) * inputs)
            pair = jnp.concatenate([acc_ref[rows, :CH], acc_ref[rows, CH:]], axis=0)
            out_ref[:, s, :] = pair.T
        for s in range(len(plan), frames):
            out_ref[:, s, :] = jnp.zeros((CH, 2 * inputs), F32)


def spectra(voltages, coefficients, carried):
    inputs, samples = voltages.shape
    frames = samples // NFFT
    small, base = twiddles()
    pair = 2 * CHUNK
    steps = NFFT // pair
    rows = len(terms(carried, frames)) * inputs
    frame_spec = lambda s: pl.BlockSpec((inputs, pair), lambda j: (0, s * steps + j))
    slot = [
        pltpu.VMEM((rows, CHUNK), BF16),
        pltpu.VMEM((rows, CHUNK), BF16),
        pltpu.VMEM((CHUNK, 2 * CH), BF16),
        pltpu.VMEM((CHUNK, 2 * CH), BF16),
    ]
    return pl.pallas_call(
        functools.partial(channelize, carried, frames, inputs),
        out_shape=jax.ShapeDtypeStruct((CH, frames, 2 * inputs), F32),
        grid=(steps,),
        in_specs=[frame_spec(s) for s in range(frames)]
        + [
            pl.BlockSpec((TAPS, pair), lambda j: (0, j)),
            pl.BlockSpec(small.shape, lambda j: (0, 0, 0)),
            pl.BlockSpec(base.shape, lambda j: (0, 0, 0)),
        ],
        out_specs=pl.BlockSpec((CH, frames, 2 * inputs), lambda j: (0, 0, 0)),
        scratch_shapes=slot + slot + [pltpu.VMEM((rows, 2 * CH), F32)],
        compiler_params=pltpu.CompilerParams(vmem_limit_bytes=48 * 2**20),
        cost_estimate=pl.CostEstimate(
            flops=6 * rows * NFFT * 2 * CH, bytes_accessed=2 * inputs * samples, transcendentals=0
        ),
        name="carried" if carried else "current",
    )(*[voltages] * frames, coefficients, small, base)


def correlate(n_time, n_input, inputs, frames, got_ref, out_ref, left_high, left_low, right_high, right_low):
    count = n_time * frames
    dot = functools.partial(jnp.dot, preferred_element_type=F32)

    @pl.when(pl.program_id(0) == 0)
    def _():
        for i in range(n_time):
            real_rows = slice(i * frames, (i + 1) * frames)
            imag_rows = slice(count + i * frames, count + (i + 1) * frames)
            for j in range(0, n_input, 2):
                lanes = slice(j * inputs, (j + 2) * inputs)
                first, second = got_ref[i * n_input + j], got_ref[i * n_input + j + 1]
                real = jnp.concatenate([first[:, :inputs], second[:, :inputs]], axis=1)
                imag = jnp.concatenate([first[:, inputs:], second[:, inputs:]], axis=1)
                real_high, real_low = split(real)
                imag_high, imag_low = split(imag)
                right_high[0, real_rows, lanes] = real_high
                right_low[0, real_rows, lanes] = real_low
                right_high[0, imag_rows, lanes] = imag_high
                right_low[0, imag_rows, lanes] = imag_low
                right_high[1, real_rows, lanes] = -imag_high
                right_low[1, real_rows, lanes] = -imag_low
                right_high[1, imag_rows, lanes] = real_high
                right_low[1, imag_rows, lanes] = real_low
        left_high[...] = right_high[0].T
        left_low[...] = right_low[0].T

    size = out_ref.shape[2]
    rows = pl.ds(pl.multiple_of(pl.program_id(0) * size, size), size)
    high, low = left_high[rows, :], left_low[rows, :]
    for part in range(2):
        total = dot(high, right_high[part]) + dot(high, right_low[part]) + dot(low, right_high[part])
        out_ref[part, 0] = total * (1.0 / count)


def visibilities(received, n_time, n_input):
    devices, frames, width = received.shape
    inputs = width // 2
    total = n_input * inputs
    depth = 2 * n_time * frames
    block = 128
    return pl.pallas_call(
        functools.partial(correlate, n_time, n_input, inputs, frames),
        out_shape=jax.ShapeDtypeStruct((2, 1, total, total), F32),
        grid=(total // block,),
        in_specs=[pl.BlockSpec(received.shape, lambda j: (0, 0, 0))],
        out_specs=pl.BlockSpec((2, 1, block, total), lambda j: (0, 0, j, 0)),
        scratch_shapes=[pltpu.VMEM((total, depth), BF16)] * 2 + [pltpu.VMEM((2, depth, total), BF16)] * 2,
        compiler_params=pltpu.CompilerParams(vmem_limit_bytes=48 * 2**20),
        name="correlate",
    )(received)


def shards(voltages, coefficients):
    n_time = lax.axis_size("tm")
    n_input = lax.axis_size("inp")
    carried = spectra(voltages, coefficients, True)
    arrived = lax.ppermute(carried, "tm", [(i, i + 1) for i in range(n_time - 1)])
    current = spectra(voltages, coefficients, False)
    outgoing = current + arrived
    received = lax.all_to_all(outgoing, ("tm", "inp"), split_axis=0, concat_axis=0, tiled=True)
    return visibilities(received, n_time, n_input)


def solution(mesh):
    in_specs = (P("inp", "tm"), P())
    out_specs = P(None, ("tm", "inp"), None, None)
    return jax.shard_map(shards, mesh=mesh, in_specs=in_specs, out_specs=out_specs, check_vma=False)
```

profile of v0, /device:TPU:1, one launch (start us, length us, event | category | flops | bytes accessed | tf_op | source)
XLA Modules:
  0.0 128.5 jit_solution(16596105844043347591)
XLA Ops:
  0.0 0.0 copy-start
  0.0 1.0 copy-done
  1.0 0.0 copy-start.1
  1.0 0.9 copy-done.1
  2.0 0.0 copy-start.2
  2.0 0.8 copy-done.2
  2.8 40.8 %carried.1 = f32[128,16,128]{2,1,0:T(8,128)S(1)} custom-call(bf16[64,131072]{1,0:T(8,128)(2,1)} %refs_15_.3, bf16[64,131072]{1,0:T(8,128)(2,1)} %refs_15_.3, bf16[64,131072]{1,0:T(8,128)(2,1)} %refs_15_.3, bf16[64,131072]{1,0:T(8,128)(2,1)} %refs_15_.3, bf16[64,131072]{1,0:T(8,128)(2,1)} %refs_15_.3, bf16[64,131072]{1,0:T(8,128)(2,1)} %refs_15_.3, ...), custom_call_target="tpu_custom_call" | custom-call | flops 12079595520 | bytes 16777216 | tf_op jit(solution)/shard_map/carried/pallas_call | solution.py:117
  43.6 4.0 %collective-permute-start = (f32[128,16,128]{2,1,0:T(8,128)S(1)}, f32[128,16,128]{2,1,0:T(8,128)S(1)}, u32[]{:S(2)}, u32[]{:S(2)}) collective-permute-start(f32[128,16,128]{2,1,0:T(8,128)S(1)} %carried.1), channel_id=1, source_target_pairs={{0,16},{16,32},{32,48},{48,64},{64,80},{80,96},{96,112},{1,17},{17... | collective-permute-start | bytes 3145736 | tf_op jit(solution)/shard_map/ppermute | solution.py:194
  47.6 43.5 %current.1 = f32[128,16,128]{2,1,0:T(8,128)S(1)} custom-call(bf16[64,131072]{1,0:T(8,128)(2,1)} %refs_15_.3, bf16[64,131072]{1,0:T(8,128)(2,1)} %refs_15_.3, bf16[64,131072]{1,0:T(8,128)(2,1)} %refs_15_.3, bf16[64,131072]{1,0:T(8,128)(2,1)} %refs_15_.3, bf16[64,131072]{1,0:T(8,128)(2,1)} %refs_15_.3, bf16[64,131072]{1,0:T(8,128)(2,1)} %refs_15_.3, ...), custom_call_target="tpu_custom_call" | custom-call | flops 12884901888 | bytes 16777216 | tf_op jit(solution)/shard_map/current/pallas_call | solution.py:117
  91.1 0.0 collective-permute-done
  91.1 0.1 add.3
  91.3 29.7 %all_to_all.5.got_ref = f32[128,16,128]{2,1,0:T(8,128)S(1)} all-to-all(f32[128,16,128]{2,1,0:T(8,128)S(1)} %add.3), channel_id=1, replica_groups=mesh['tm'=8,'inp'=16] {'tm','inp'}, dimensions={0} | all-to-all | bytes 2097152 | tf_op jit(solution)/shard_map/all_to_all | solution.py:197
  120.9 7.5 %correlate.1 = f32[2,1,1024,1024]{3,2,1,0:T(8,128)} custom-call(f32[128,16,128]{2,1,0:T(8,128)S(1)} %all_to_all.5.got_ref), custom_call_target="tpu_custom_call" | custom-call | tf_op jit(solution)/shard_map/correlate/pallas_call | solution.py:178
Async XLA Ops:
  0.0 1.0 copy-start
  1.0 0.9 copy-start.1
  2.0 0.8 copy-start.2
  43.6 47.6 %collective-permute-start = (f32[128,16,128]{2,1,0:T(8,128)S(1)}, f32[128,16,128]{2,1,0:T(8,128)S(1)}, u32[]{:S(2)}, u32[]{:S(2)}) collective-permute-start(f32[128,16,128]{2,1,0:T(8,128)S(1)} %carried.1), channel_id=1, source_target_pairs={{0,16},{16,32},{32,48},{48,64},{64,80},{80,96},{96,112},{1,17},{17... | collective-permute-start | bytes 3145736 | tf_op jit(solution)/shard_map/ppermute | solution.py:194
where the time goes:
time: 129 us; the launch traced here: 128 us
  Pallas kernels  91.9 us (71%)
  blocking collectives  29.7 us (23%)
  starting transfers between devices  4 us (3%)
  local copies, waits for them, and re-layouts  2.75 us (2%)
    pallas_call x2, Pallas kernels, spectra(): pl.pallas_call(functools.partial(channelize, carried, frames, inputs), ou...  84.4 us
    all_to_all x1, blocking collectives, shards(): lax.all_to_all(outgoing, ('tm', 'inp'), split_axis=0, concat_axis=0, tile...  29.7 us
    pallas_call x1, Pallas kernels, visibilities(): pl.pallas_call(functools.partial(correlate, n_time, n_input, inputs, fram...  7.52 us
    ppermute x1, starting transfers between devices, shards(): lax.ppermute(carried, 'tm', [(i, i + 1) for i in range(n_time - 1)])  4 us
    unnamed x6, local copies, waits for them, and re-layouts  2.75 us
  transfers between devices with their start and end apart: 1, of which 0 were waited for; matrix products, arithmetic and copies ran while one was open for 0% of the time, Pallas kernels for 34%

commit v1 on v0

v1 whole, which is shorter than its diff:
```python
import functools

import jax
import jax.numpy as jnp
import numpy as np
from jax import lax
from jax.experimental import pallas as pl
from jax.experimental.pallas import tpu as pltpu
from jax.sharding import PartitionSpec as P

NFFT = 8192
TAPS = 16
CH = 128
CH0 = 1024
LANES = 128
CHUNK = 256
HALF = NFFT // 2
GROUP = 8
DEPTH = 1
F32 = jnp.float32
BF16 = jnp.bfloat16


def twiddles():
    channel = (CH0 + np.arange(CH)).reshape(CH // 2, 2).T
    small = 2.0 * np.pi / NFFT * (np.arange(CHUNK)[:, None] * channel[:, None, :] % NFFT)
    base = 2.0 * np.pi / NFFT * (np.arange(HALF // CHUNK)[:, None, None] * CHUNK * channel % NFFT)
    real, imag = np.cos(small) * NFFT ** (-0.5), -np.sin(small) * NFFT ** (-0.5)
    turn_real, turn_imag = np.cos(base), -np.sin(base)
    small = np.stack([np.concatenate([real, imag], axis=-1), np.concatenate([-imag, real], axis=-1)])
    base = np.stack([np.concatenate([turn_real] * 2, axis=-1), np.concatenate([turn_imag] * 2, axis=-1)], axis=1)
    return jnp.asarray(small, F32), jnp.asarray(base, F32)


def split(value):
    high = value.astype(BF16)
    return high, (value - high.astype(F32)).astype(BF16)


def toeplitz_tree(coefficients, depth):
    size = (len(coefficients) + 1) // 2
    if depth == 0 or size == 1:
        return coefficients
    half = size // 2
    upper, middle, lower = (coefficients[k : k + size - 1] for k in (0, half, size))
    above = [a - b for a, b in zip(upper, middle)]
    below = [a - b for a, b in zip(lower, middle)]
    return [toeplitz_tree(part, depth - 1) for part in (middle, above, below)]


def flatten(tree):
    return [leaf for part in tree for leaf in flatten(part)] if isinstance(tree, list) else [tree]


def rebuild(tree, leaves):
    return [rebuild(part, leaves) for part in tree] if isinstance(tree, list) else next(leaves)


def weighted(pairs):
    total = None
    for coefficient, sample in pairs:
        product = coefficient * sample
        total = product if total is None else total + product
    return total


def toeplitz(tree, samples):
    size = len(samples)
    if len(tree) == 2 * size - 1 and not isinstance(tree[0], list):
        return [weighted((tree[size - 1 + i - j], samples[j]) for j in range(size)) for i in range(size)]
    half = size // 2
    first, second = samples[:half], samples[half:]
    both = toeplitz(tree[0], [a + b for a, b in zip(first, second)])
    above = toeplitz(tree[1], second)
    below = toeplitz(tree[2], first)
    return [a + b for a, b in zip(both, above)] + [a + b for a, b in zip(both, below)]


def coefficient_tree(taps):
    half = TAPS // 2
    return [list(taps), toeplitz_tree(list(taps[1:]), DEPTH)]


def later_frames(tree, x):
    taps, middle = tree
    half = TAPS // 2
    inner = toeplitz(middle, x[half:])
    first = [weighted((taps[TAPS + s - j], x[j]) for j in range(s + 1, half)) for s in range(half - 1)]
    second = [weighted((taps[TAPS + s - j], x[j + half]) for j in range(s + 1, half)) for s in range(half - 1)]
    return [a + b for a, b in zip(inner, first)] + [inner[half - 1]] + second


def these_frames(tree, x):
    taps, middle = tree
    half = TAPS // 2
    inner = toeplitz(middle, x[:half])
    first = [weighted((taps[s - j], x[j]) for j in range(s + 1)) for s in range(half)]
    second = [weighted((taps[s - j], x[j + half]) for j in range(s + 1)) for s in range(half)]
    return first + [a + b for a, b in zip(second, inner)]


def channelize(carried, frames, inputs, *refs):
    x_refs = refs[:frames], refs[frames : 2 * frames]
    h_refs, (small_ref, base_ref, out_ref, acc_ref) = refs[2 * frames : 2 * frames + 2], refs[2 * frames + 2 :]
    step = pl.program_id(0)
    groups = inputs // GROUP

    @pl.when(step == 0)
    def _():
        acc_ref[...] = jnp.zeros_like(acc_ref)

    lines = [[], []]
    trees = []
    for block in range(CHUNK // LANES):
        lanes = slice(block * LANES, (block + 1) * LANES)
        trees.append([])
        for h_ref in h_refs:
            taps = [jnp.broadcast_to(h_ref[t : t + 1, lanes], (GROUP, LANES)) for t in range(TAPS)]
            trees[-1].append(coefficient_tree(taps))
    for group in range(groups):
        at = slice(group * GROUP, (group + 1) * GROUP)
        columns = [[], []]
        for block in range(CHUNK // LANES):
            lanes = slice(block * LANES, (block + 1) * LANES)
            first, second = (
                (later_frames if carried else these_frames)(tree, [ref[at, lanes].astype(F32) for ref in x])
                for tree, x in zip(trees[block], x_refs)
            )
            for parity in range(2):
                values = [a - b if parity else a + b for a, b in zip(first, second)]
                if carried:
                    values.append(jnp.zeros((GROUP, LANES), F32))
                pieces = [split(jnp.concatenate(values[s : s + 2], axis=0)) for s in range(0, frames, 2)]
                columns[parity].append(
                    jnp.concatenate([p[0] for p in pieces] + [p[1] for p in pieces], axis=0)
                )
        for parity in range(2):
            lines[parity].append(jnp.concatenate(columns[parity], axis=1))

    for parity in range(2):
        table = small_ref[0, parity] * base_ref[step, 0, parity : parity + 1]
        table = table + small_ref[1, parity] * base_ref[step, 1, parity : parity + 1]
        total = jnp.dot(
            jnp.concatenate(lines[parity], axis=0),
            jnp.concatenate(split(table), axis=1),
            preferred_element_type=F32,
        )
        rows = frames * GROUP
        for group in range(groups):
            high = total[2 * group * rows : (2 * group + 1) * rows]
            low = total[(2 * group + 1) * rows : (2 * group + 2) * rows]
            acc_ref[parity, group * rows : (group + 1) * rows] += high + low

    @pl.when(step == pl.num_programs(0) - 1)
    def _():
        half = CH // 2
        for s in range(frames):
            sums = []
            for parity in range(2):
                starts = [(group * frames + s) * GROUP for group in range(groups)]
                whole = jnp.concatenate([acc_ref[parity, start : start + GROUP] for start in starts], axis=0)
                sums.append(whole[:, :CH] + whole[:, CH:])
            real = jnp.concatenate([part[:, :half] for part in sums], axis=1)
            imag = jnp.concatenate([part[:, half:] for part in sums], axis=1)
            turned = jnp.concatenate([real, imag], axis=0).T
            for parity in range(2):
                out_ref[:, parity, s, :] = turned[parity * half : (parity + 1) * half]


def spectra(voltages, coefficients, carried):
    inputs, samples = voltages.shape
    frames = samples // NFFT
    small, base = twiddles()
    steps = HALF // CHUNK
    rows = frames * inputs
    frame_spec = lambda s, part: pl.BlockSpec((inputs, CHUNK), lambda j: (0, (2 * s + part) * steps + j))
    out = pl.pallas_call(
        functools.partial(channelize, carried, frames, inputs),
        out_shape=jax.ShapeDtypeStruct((CH // 2, 2, frames, 2 * inputs), F32),
        grid=(steps,),
        in_specs=[frame_spec(s, part) for part in range(2) for s in range(frames)]
        + [
            pl.BlockSpec((TAPS, CHUNK), lambda j: (0, j)),
            pl.BlockSpec((TAPS, CHUNK), lambda j: (0, steps + j)),
            pl.BlockSpec(small.shape, lambda j: (0, 0, 0, 0)),
            pl.BlockSpec(base.shape, lambda j: (0, 0, 0, 0)),
        ],
        out_specs=pl.BlockSpec((CH // 2, 2, frames, 2 * inputs), lambda j: (0, 0, 0, 0)),
        scratch_shapes=[pltpu.VMEM((2, rows, 2 * CH), F32)],
        compiler_params=pltpu.CompilerParams(vmem_limit_bytes=48 * 2**20),
        cost_estimate=pl.CostEstimate(
            flops=4 * rows * NFFT * 2 * CH, bytes_accessed=2 * inputs * samples, transcendentals=0
        ),
        name="carried" if carried else "current",
    )(*[voltages] * (2 * frames), coefficients, coefficients, small, base)
    return out.reshape(CH, frames, 2 * inputs)


def correlate(n_time, n_input, inputs, frames, got_ref, out_ref, left_high, left_low, right_high, right_low):
    count = n_time * frames
    dot = functools.partial(jnp.dot, preferred_element_type=F32)

    @pl.when(pl.program_id(0) == 0)
    def _():
        for i in range(n_time):
            real_rows = slice(i * frames, (i + 1) * frames)
            imag_rows = slice(count + i * frames, count + (i + 1) * frames)
            for j in range(0, n_input, 2):
                lanes = slice(j * inputs, (j + 2) * inputs)
                first, second = got_ref[i * n_input + j], got_ref[i * n_input + j + 1]
                real = jnp.concatenate([first[:, :inputs], second[:, :inputs]], axis=1)
                imag = jnp.concatenate([first[:, inputs:], second[:, inputs:]], axis=1)
                real_high, real_low = split(real)
                imag_high, imag_low = split(imag)
                right_high[0, real_rows, lanes] = real_high
                right_low[0, real_rows, lanes] = real_low
                right_high[0, imag_rows, lanes] = imag_high
                right_low[0, imag_rows, lanes] = imag_low
                right_high[1, real_rows, lanes] = -imag_high
                right_low[1, real_rows, lanes] = -imag_low
                right_high[1, imag_rows, lanes] = real_high
                right_low[1, imag_rows, lanes] = real_low
        left_high[...] = right_high[0].T
        left_low[...] = right_low[0].T

    size = out_ref.shape[2]
    rows = pl.ds(pl.multiple_of(pl.program_id(0) * size, size), size)
    high, low = left_high[rows, :], left_low[rows, :]
    for part in range(2):
        total = dot(high, right_high[part]) + dot(high, right_low[part]) + dot(low, right_high[part])
        out_ref[part, 0] = total * (1.0 / count)


def visibilities(received, n_time, n_input):
    devices, frames, width = received.shape
    inputs = width // 2
    total = n_input * inputs
    depth = 2 * n_time * frames
    block = 128
    return pl.pallas_call(
        functools.partial(correlate, n_time, n_input, inputs, frames),
        out_shape=jax.ShapeDtypeStruct((2, 1, total, total), F32),
        grid=(total // block,),
        in_specs=[pl.BlockSpec(received.shape, lambda j: (0, 0, 0))],
        out_specs=pl.BlockSpec((2, 1, block, total), lambda j: (0, 0, j, 0)),
        scratch_shapes=[pltpu.VMEM((total, depth), BF16)] * 2 + [pltpu.VMEM((2, depth, total), BF16)] * 2,
        compiler_params=pltpu.CompilerParams(vmem_limit_bytes=48 * 2**20),
        name="correlate",
    )(received)


def shards(voltages, coefficients):
    n_time = lax.axis_size("tm")
    n_input = lax.axis_size("inp")
    carried = spectra(voltages, coefficients, True)
    arrived = lax.ppermute(carried, "tm", [(i, i + 1) for i in range(n_time - 1)])
    current = spectra(voltages, coefficients, False)
    outgoing = current + arrived
    received = lax.all_to_all(outgoing, ("tm", "inp"), split_axis=0, concat_axis=0, tiled=True)
    return visibilities(received, n_time, n_input)


def solution(mesh):
    in_specs = (P("inp", "tm"), P())
    out_specs = P(None, ("tm", "inp"), None, None)
    return jax.shard_map(shards, mesh=mesh, in_specs=in_specs, out_specs=out_specs, check_vma=False)
```

time: 129 us -> 125 us (0.969)
  Pallas kernels: 91.9 us -> 87 us
    pallas_call x2, Pallas kernels: 84.4 us -> 79.5 us  [spectra(): pl.pallas_call(functools.partial(channelize, carried, frames, inputs), ou...]
  transfers between devices with their start and end apart: 1 -> 1, of which waited for: 0 -> 0; matrix products, arithmetic and copies ran while one was open for 0% -> 0% of each run, Pallas kernels for 34% -> 33%
where the time goes in v1:
time: 125 us
  Pallas kernels  87 us (70%)
  blocking collectives  28.8 us (23%)
  starting transfers between devices  4.91 us (4%)
  local copies, waits for them, and re-layouts  2.84 us (2%)
  other arithmetic  1.32 us (1%)
    pallas_call x2, Pallas kernels, spectra(): pl.pallas_call(functools.partial(channelize, carried, frames, inputs), ou...  79.5 us
    all_to_all x1, blocking collectives, shards(): lax.all_to_all(outgoing, ('tm', 'inp'), split_axis=0, concat_axis=0, tile...  28.8 us
    pallas_call x1, Pallas kernels, visibilities(): pl.pallas_call(functools.partial(correlate, n_time, n_input, inputs, fram...  7.53 us
    ppermute x1, starting transfers between devices, shards(): lax.ppermute(carried, 'tm', [(i, i + 1) for i in range(n_time - 1)])  4.91 us
    unnamed x6, local copies, waits for them, and re-layouts  2.84 us
  transfers between devices with their start and end apart: 1, of which 0 were waited for; matrix products, arithmetic and copies ran while one was open for 0% of the time, Pallas kernels for 33%

profile of v1, /device:TPU:1, one launch (start us, length us, event | category | flops | bytes accessed | tf_op | source)
XLA Modules:
  0.0 124.9 jit_solution(8418076242607101858)
XLA Ops:
  0.0 0.0 copy-start
  0.0 1.0 copy-done
  1.0 0.0 copy-start.1
  1.0 1.0 copy-done.1
  2.1 0.0 copy-start.2
  2.1 0.8 copy-done.2
  2.8 38.6 %carried.1 = f32[64,2,16,128]{3,2,1,0:T(8,128)} custom-call(bf16[64,131072]{1,0:T(8,128)(2,1)} %refs_31_.3, bf16[64,131072]{1,0:T(8,128)(2,1)} %refs_31_.3, bf16[64,131072]{1,0:T(8,128)(2,1)} %refs_31_.3, bf16[64,131072]{1,0:T(8,128)(2,1)} %refs_31_.3, bf16[64,131072]{1,0:T(8,128)(2,1)} %refs_31_.3, bf16[64,131072]{1,0:T(8,128)(2,1)} %refs_31_.3, ...), custom_call_target="tpu_custom_call" | custom-call | flops 8589934592 | bytes 16777216 | tf_op jit(solution)/shard_map/carried/pallas_call | solution.py:177
  41.4 4.9 %collective-permute-start = (f32[128,16,128]{2,1,0:T(8,128)}, f32[128,16,128]{2,1,0:T(8,128)}, u32[]{:S(2)}, u32[]{:S(2)}) collective-permute-start(f32[128,16,128]{2,1,0:T(8,128)} %bitcast.1), channel_id=1, source_target_pairs={{0,16},{16,32},{32,48},{48,64},{64,80},{80,96},{96,112},{1,17},{17... | collective-permute-start | bytes 3145736 | tf_op jit(solution)/shard_map/ppermute | solution.py:256
  46.3 40.9 %current.1 = f32[64,2,16,128]{3,2,1,0:T(8,128)S(1)} custom-call(bf16[64,131072]{1,0:T(8,128)(2,1)} %refs_31_.3, bf16[64,131072]{1,0:T(8,128)(2,1)} %refs_31_.3, bf16[64,131072]{1,0:T(8,128)(2,1)} %refs_31_.3, bf16[64,131072]{1,0:T(8,128)(2,1)} %refs_31_.3, bf16[64,131072]{1,0:T(8,128)(2,1)} %refs_31_.3, bf16[64,131072]{1,0:T(8,128)(2,1)} %refs_31_.3, ...), custom_call_target="tpu_custom_call" | custom-call | flops 8589934592 | bytes 16777216 | tf_op jit(solution)/shard_map/current/pallas_call | solution.py:177
  87.2 0.0 collective-permute-done
  87.2 1.3 %bitcast_add_fusion = f32[128,16,128]{2,1,0:T(8,128)S(1)} fusion(f32[128,16,128]{2,1,0:T(8,128)} %collective-permute-done, f32[64,2,16,128]{3,2,1,0:T(8,128)S(1)} %current.1), kind=kLoop, calls=%fused_computation | loop fusion | flops 262144 | bytes 3145728 | tf_op jit(solution)/shard_map/add | solution.py:258
  88.6 28.8 %all_to_all.5.got_ref = f32[128,16,128]{2,1,0:T(8,128)S(1)} all-to-all(f32[128,16,128]{2,1,0:T(8,128)S(1)} %bitcast_add_fusion), channel_id=1, replica_groups=mesh['tm'=8,'inp'=16] {'tm','inp'}, dimensions={0} | all-to-all | bytes 2097152 | tf_op jit(solution)/shard_map/all_to_all | solution.py:259
  117.4 7.5 %correlate.1 = f32[2,1,1024,1024]{3,2,1,0:T(8,128)} custom-call(f32[128,16,128]{2,1,0:T(8,128)S(1)} %all_to_all.5.got_ref), custom_call_target="tpu_custom_call" | custom-call | tf_op jit(solution)/shard_map/correlate/pallas_call | solution.py:240
Async XLA Ops:
  0.0 1.0 copy-start
  1.0 1.0 copy-start.1
  2.1 0.8 copy-start.2
  41.4 45.8 %collective-permute-start = (f32[128,16,128]{2,1,0:T(8,128)}, f32[128,16,128]{2,1,0:T(8,128)}, u32[]{:S(2)}, u32[]{:S(2)}) collective-permute-start(f32[128,16,128]{2,1,0:T(8,128)} %bitcast.1), channel_id=1, source_target_pairs={{0,16},{16,32},{32,48},{48,64},{64,80},{80,96},{96,112},{1,17},{17... | collective-permute-start | bytes 3145736 | tf_op jit(solution)/shard_map/ppermute | solution.py:256

commit v2 on v1

--- a/solution.py
+++ b/solution.py
@@ -13,23 +13,29 @@
 CH = 128
 CH0 = 1024
 LANES = 128
-CHUNK = 256
+CHUNK = 512
 HALF = NFFT // 2
 GROUP = 8
-DEPTH = 1
+FINE = 16
+DEPTH = 2
 F32 = jnp.float32
 BF16 = jnp.bfloat16
 
 
+def turns(samples):
+    channel = (CH0 + np.arange(CH)).reshape(CH // 2, 2).T
+    angle = 2.0 * np.pi / NFFT * (samples[:, None, None] * channel % NFFT)
+    return np.cos(angle), -np.sin(angle)
+
+
 def twiddles():
-    channel = (CH0 + np.arange(CH)).reshape(CH // 2, 2).T
-    small = 2.0 * np.pi / NFFT * (np.arange(CHUNK)[:, None] * channel[:, None, :] % NFFT)
-    base = 2.0 * np.pi / NFFT * (np.arange(HALF // CHUNK)[:, None, None] * CHUNK * channel % NFFT)
-    real, imag = np.cos(small) * NFFT ** (-0.5), -np.sin(small) * NFFT ** (-0.5)
-    turn_real, turn_imag = np.cos(base), -np.sin(base)
-    small = np.stack([np.concatenate([real, imag], axis=-1), np.concatenate([-imag, real], axis=-1)])
-    base = np.stack([np.concatenate([turn_real] * 2, axis=-1), np.concatenate([turn_imag] * 2, axis=-1)], axis=1)
-    return jnp.asarray(small, F32), jnp.asarray(base, F32)
+    real, imag = (part.transpose(1, 0, 2) * NFFT ** (-0.5) for part in turns(np.arange(FINE)))
+    fine = np.stack([np.concatenate([real, imag], axis=-1), np.concatenate([-imag, real], axis=-1)])
+    coarse, base = (
+        np.stack([np.concatenate([part] * 2, axis=-1) for part in turns(samples)], axis=1)
+        for samples in (np.arange(0, CHUNK, FINE), np.arange(0, HALF, CHUNK))
+    )
+    return jnp.asarray(np.concatenate([part.reshape(-1, CH) for part in (fine, coarse, base)]), F32)
 
 
 def split(value):
@@ -57,11 +63,10 @@
 
 
 def weighted(pairs):
-    total = None
-    for coefficient, sample in pairs:
-        product = coefficient * sample
-        total = product if total is None else total + product
-    return total
+    parts = [coefficient * sample for coefficient, sample in pairs]
+    while len(parts) > 1:
+        parts = [parts[k] + parts[k + 1] if k + 1 < len(parts) else parts[k] for k in range(0, len(parts), 2)]
+    return parts[0]
 
 
 def toeplitz(tree, samples):
@@ -99,15 +104,22 @@
     return first + [a + b for a, b in zip(second, inner)]
 
 
-def channelize(carried, frames, inputs, *refs):
-    x_refs = refs[:frames], refs[frames : 2 * frames]
-    h_refs, (small_ref, base_ref, out_ref, acc_ref) = refs[2 * frames : 2 * frames + 2], refs[2 * frames + 2 :]
+def channelize(carried, frames, inputs, x_ref, h_first, h_second, table_ref, out_ref, acc_ref, small_ref):
+    h_refs = h_first, h_second
     step = pl.program_id(0)
     groups = inputs // GROUP
+    turn = lambda start, part, parity: table_ref[pl.ds(start + 2 * part + parity, 1), :]
 
     @pl.when(step == 0)
     def _():
         acc_ref[...] = jnp.zeros_like(acc_ref)
+        for parity in range(2):
+            real, imag = (table_ref[(2 * part + parity) * FINE : (2 * part + parity + 1) * FINE] for part in range(2))
+            for k in range(CHUNK // FINE):
+                at = slice(k * FINE, (k + 1) * FINE)
+                turn_real, turn_imag = (turn(4 * FINE + 4 * k, part, parity) for part in range(2))
+                small_ref[0, parity, at] = real * turn_real + imag * turn_imag
+                small_ref[1, parity, at] = imag * turn_real - real * turn_imag
 
     lines = [[], []]
     trees = []
@@ -118,13 +130,13 @@
             taps = [jnp.broadcast_to(h_ref[t : t + 1, lanes], (GROUP, LANES)) for t in range(TAPS)]
             trees[-1].append(coefficient_tree(taps))
     for group in range(groups):
-        at = slice(group * GROUP, (group + 1) * GROUP)
         columns = [[], []]
         for block in range(CHUNK // LANES):
-            lanes = slice(block * LANES, (block + 1) * LANES)
             first, second = (
-                (later_frames if carried else these_frames)(tree, [ref[at, lanes].astype(F32) for ref in x])
-                for tree, x in zip(trees[block], x_refs)
+                (later_frames if carried else these_frames)(
+                    trees[block][part], [x_ref[group, s, part, block].astype(F32) for s in range(frames)]
+                )
+                for part in range(2)
             )
             for parity in range(2):
                 values = [a - b if parity else a + b for a, b in zip(first, second)]
@@ -138,8 +150,8 @@
             lines[parity].append(jnp.concatenate(columns[parity], axis=1))
 
     for parity in range(2):
-        table = small_ref[0, parity] * base_ref[step, 0, parity : parity + 1]
-        table = table + small_ref[1, parity] * base_ref[step, 1, parity : parity + 1]
+        start = 4 * FINE + 4 * (CHUNK // FINE) + 4 * step
+        table = small_ref[0, parity] * turn(start, 0, parity) + small_ref[1, parity] * turn(start, 1, parity)
         total = jnp.dot(
             jnp.concatenate(lines[parity], axis=0),
             jnp.concatenate(split(table), axis=1),
@@ -153,47 +165,64 @@
 
     @pl.when(step == pl.num_programs(0) - 1)
     def _():
-        half = CH // 2
-        for s in range(frames):
-            sums = []
-            for parity in range(2):
-                starts = [(group * frames + s) * GROUP for group in range(groups)]
-                whole = jnp.concatenate([acc_ref[parity, start : start + GROUP] for start in starts], axis=0)
-                sums.append(whole[:, :CH] + whole[:, CH:])
-            real = jnp.concatenate([part[:, :half] for part in sums], axis=1)
-            imag = jnp.concatenate([part[:, half:] for part in sums], axis=1)
-            turned = jnp.concatenate([real, imag], axis=0).T
-            for parity in range(2):
-                out_ref[:, parity, s, :] = turned[parity * half : (parity + 1) * half]
+        for parity in range(2):
+            out_ref[parity] = acc_ref[parity, :, :CH] + acc_ref[parity, :, CH:]
+
+
+def assemble(frames, inputs, here_ref, before_ref, out_ref):
+    groups = inputs // GROUP
+    half = CH // 2
+    for s in range(frames):
+        sums = []
+        for parity in range(2):
+            spans = [slice((group * frames + s) * GROUP, (group * frames + s + 1) * GROUP) for group in range(groups)]
+            sums.append(
+                jnp.concatenate([here_ref[parity, span] + before_ref[parity, span] for span in spans], axis=0)
+            )
+        real = jnp.concatenate([part[:, :half] for part in sums], axis=1)
+        imag = jnp.concatenate([part[:, half:] for part in sums], axis=1)
+        turned = jnp.concatenate([real, imag], axis=0).T
+        for parity in range(2):
+            out_ref[:, parity, s, :] = turned[parity * half : (parity + 1) * half]
+
+
+def messages(here, before, inputs):
+    frames = here.shape[1] // inputs
+    return pl.pallas_call(
+        functools.partial(assemble, frames, inputs),
+        out_shape=jax.ShapeDtypeStruct((CH // 2, 2, frames, 2 * inputs), F32),
+        compiler_params=pltpu.CompilerParams(vmem_limit_bytes=16 * 2**20),
+        name="messages",
+    )(here, before).reshape(CH, frames, 2 * inputs)
 
 
 def spectra(voltages, coefficients, carried):
     inputs, samples = voltages.shape
     frames = samples // NFFT
-    small, base = twiddles()
+    table, coefficients = (pltpu.with_memory_space_constraint(part, pltpu.HBM) for part in (twiddles(), coefficients))
     steps = HALF // CHUNK
     rows = frames * inputs
-    frame_spec = lambda s, part: pl.BlockSpec((inputs, CHUNK), lambda j: (0, (2 * s + part) * steps + j))
-    out = pl.pallas_call(
+    tiles = voltages.reshape(inputs // GROUP, GROUP, samples // LANES, LANES).transpose(0, 2, 1, 3)
+    tiles = tiles.reshape(inputs // GROUP, frames, 2, HALF // LANES, GROUP, LANES)
+    block = (inputs // GROUP, frames, 2, CHUNK // LANES, GROUP, LANES)
+    return pl.pallas_call(
         functools.partial(channelize, carried, frames, inputs),
-        out_shape=jax.ShapeDtypeStruct((CH // 2, 2, frames, 2 * inputs), F32),
+        out_shape=jax.ShapeDtypeStruct((2, rows, CH), F32),
         grid=(steps,),
-        in_specs=[frame_spec(s, part) for part in range(2) for s in range(frames)]
-        + [
+        in_specs=[
+            pl.BlockSpec(block, lambda j: (0, 0, 0, j, 0, 0)),
             pl.BlockSpec((TAPS, CHUNK), lambda j: (0, j)),
             pl.BlockSpec((TAPS, CHUNK), lambda j: (0, steps + j)),
-            pl.BlockSpec(small.shape, lambda j: (0, 0, 0, 0)),
-            pl.BlockSpec(base.shape, lambda j: (0, 0, 0, 0)),
+            pl.BlockSpec(table.shape, lambda j: (0, 0)),
         ],
-        out_specs=pl.BlockSpec((CH // 2, 2, frames, 2 * inputs), lambda j: (0, 0, 0, 0)),
-        scratch_shapes=[pltpu.VMEM((2, rows, 2 * CH), F32)],
+        out_specs=pl.BlockSpec((2, rows, CH), lambda j: (0, 0, 0)),
+        scratch_shapes=[pltpu.VMEM((2, rows, 2 * CH), F32), pltpu.VMEM((2, 2, CHUNK, CH), F32)],
         compiler_params=pltpu.CompilerParams(vmem_limit_bytes=48 * 2**20),
         cost_estimate=pl.CostEstimate(
             flops=4 * rows * NFFT * 2 * CH, bytes_accessed=2 * inputs * samples, transcendentals=0
         ),
         name="carried" if carried else "current",
-    )(*[voltages] * (2 * frames), coefficients, coefficients, small, base)
-    return out.reshape(CH, frames, 2 * inputs)
+    )(tiles, coefficients, coefficients, table)
 
 
 def correlate(n_time, n_input, inputs, frames, got_ref, out_ref, left_high, left_low, right_high, right_low):
@@ -255,7 +284,7 @@
     carried = spectra(voltages, coefficients, True)
     arrived = lax.ppermute(carried, "tm", [(i, i + 1) for i in range(n_time - 1)])
     current = spectra(voltages, coefficients, False)
-    outgoing = current + arrived
+    outgoing = messages(current, arrived, voltages.shape[0])
     received = lax.all_to_all(outgoing, ("tm", "inp"), split_axis=0, concat_axis=0, tiled=True)
     return visibilities(received, n_time, n_input)
 

time: 125 us -> 96.8 us (0.77)
  Pallas kernels: 87 us -> 63 us
  local copies, waits for them, and re-layouts: 2.84 us -> 0 us
  other arithmetic: 1.32 us -> 0 us
    pallas_call x2, Pallas kernels: 79.5 us -> 54.3 us  [spectra(): pl.pallas_call(functools.partial(channelize, carried, frames, inputs), ou...]
    unnamed x6 -> x0, local copies, waits for them, and re-layouts: 2.84 us -> none
    add x1 -> x0, other arithmetic: 1.32 us -> none  [shards(): outgoing = current + arrived]
  transfers between devices with their start and end apart: 1 -> 1, of which waited for: 0 -> 0; matrix products, arithmetic and copies ran while one was open for 0% -> 0% of each run, Pallas kernels for 33% -> 30%
where the time goes in v2:
time: 96.8 us; the launch traced here: 96.7 us
  Pallas kernels  63 us (65%)
  blocking collectives  29.7 us (31%)
  starting transfers between devices  4 us (4%)
    pallas_call x2, Pallas kernels, spectra(): pl.pallas_call(functools.partial(channelize, carried, frames, inputs), ou...  54.3 us
    all_to_all x1, blocking collectives, shards(): lax.all_to_all(outgoing, ('tm', 'inp'), split_axis=0, concat_axis=0, tile...  29.7 us
    pallas_call x1, Pallas kernels, visibilities(): pl.pallas_call(functools.partial(correlate, n_time, n_input, inputs, fram...  7.53 us
    ppermute x1, starting transfers between devices, shards(): lax.ppermute(carried, 'tm', [(i, i + 1) for i in range(n_time - 1)])  4 us
  transfers between devices with their start and end apart: 1, of which 0 were waited for; matrix products, arithmetic and copies ran while one was open for 0% of the time, Pallas kernels for 30%

profile of v2, /device:TPU:1, one launch (start us, length us, event | category | flops | bytes accessed | tf_op | source)
XLA Modules:
  0.0 96.7 jit_solution(3886503979412442991)
XLA Ops:
  0.0 25.5 %carried.1 = f32[2,1024,128]{2,1,0:T(8,128)S(1)} custom-call(bf16[8,16,2,32,8,128]{5,4,3,2,1,0:T(8,128)(2,1)} %bitcast.7, f32[16,8192]{1,0:T(8,128)} %h_second.3, f32[16,8192]{1,0:T(8,128)} %h_second.3, f32[224,128]{1,0:T(8,128)} %constant.2.clone.table_ref), custom_call_target="tpu_custom_call" | custom-call | flops 8589934592 | bytes 16777216 | tf_op jit(solution)/shard_map/carried/pallas_call | solution.py:208
  25.5 4.0 %collective-permute-start = (f32[2,1024,128]{2,1,0:T(8,128)S(1)}, f32[2,1024,128]{2,1,0:T(8,128)S(1)}, u32[]{:S(2)}, u32[]{:S(2)}) collective-permute-start(f32[2,1024,128]{2,1,0:T(8,128)S(1)} %carried.1), channel_id=1, source_target_pairs={{0,16},{16,32},{32,48},{48,64},{64,80},{80,96},{96,112},{1,17},{17... | collective-permute-start | bytes 3145736 | tf_op jit(solution)/shard_map/ppermute | solution.py:285
  29.6 28.8 %current.1.here_ref = f32[2,1024,128]{2,1,0:T(8,128)S(1)} custom-call(bf16[8,16,2,32,8,128]{5,4,3,2,1,0:T(8,128)(2,1)} %bitcast.8, f32[16,8192]{1,0:T(8,128)} %h_second.3, f32[16,8192]{1,0:T(8,128)} %h_second.3, f32[224,128]{1,0:T(8,128)} %constant.2.clone.table_ref), custom_call_target="tpu_custom_call" | custom-call | flops 8589934592 | bytes 16777216 | tf_op jit(solution)/shard_map/current/pallas_call | solution.py:208
  58.4 0.0 collective-permute-done.before_ref
  58.4 1.1 %messages.1 = f32[64,2,16,128]{3,2,1,0:T(8,128)S(1)} custom-call(f32[2,1024,128]{2,1,0:T(8,128)S(1)} %current.1.here_ref, f32[2,1024,128]{2,1,0:T(8,128)S(1)} %collective-permute-done.before_ref), custom_call_target="tpu_custom_call" | custom-call | tf_op jit(solution)/shard_map/messages/pallas_call | solution.py:191
  59.5 29.7 %all_to_all.5.got_ref = f32[128,16,128]{2,1,0:T(8,128)S(1)} all-to-all(f32[128,16,128]{2,1,0:T(8,128)S(1)} %bitcast.6), channel_id=1, replica_groups=mesh['tm'=8,'inp'=16] {'tm','inp'}, dimensions={0} | all-to-all | bytes 2097152 | tf_op jit(solution)/shard_map/all_to_all | solution.py:288
  89.2 7.5 %correlate.1 = f32[2,1,1024,1024]{3,2,1,0:T(8,128)} custom-call(f32[128,16,128]{2,1,0:T(8,128)S(1)} %all_to_all.5.got_ref), custom_call_target="tpu_custom_call" | custom-call | tf_op jit(solution)/shard_map/correlate/pallas_call | solution.py:269
Async XLA Ops:
  25.5 32.8 %collective-permute-start = (f32[2,1024,128]{2,1,0:T(8,128)S(1)}, f32[2,1024,128]{2,1,0:T(8,128)S(1)}, u32[]{:S(2)}, u32[]{:S(2)}) collective-permute-start(f32[2,1024,128]{2,1,0:T(8,128)S(1)} %carried.1), channel_id=1, source_target_pairs={{0,16},{16,32},{32,48},{48,64},{64,80},{80,96},{96,112},{1,17},{17... | collective-permute-start | bytes 3145736 | tf_op jit(solution)/shard_map/ppermute | solution.py:285

commit v3 on v2

--- a/solution.py
+++ b/solution.py
@@ -17,6 +17,8 @@
 HALF = NFFT // 2
 GROUP = 8
 FINE = 16
+TILE = 512
+SPAN = 8
 DEPTH = 2
 F32 = jnp.float32
 BF16 = jnp.bfloat16
@@ -52,14 +54,6 @@
     above = [a - b for a, b in zip(upper, middle)]
     below = [a - b for a, b in zip(lower, middle)]
     return [toeplitz_tree(part, depth - 1) for part in (middle, above, below)]
-
-
-def flatten(tree):
-    return [leaf for part in tree for leaf in flatten(part)] if isinstance(tree, list) else [tree]
-
-
-def rebuild(tree, leaves):
-    return [rebuild(part, leaves) for part in tree] if isinstance(tree, list) else next(leaves)
 
 
 def weighted(pairs):
@@ -83,45 +77,75 @@
 
 def coefficient_tree(taps):
     half = TAPS // 2
-    return [list(taps), toeplitz_tree(list(taps[1:]), DEPTH)]
+    taps = list(taps)
+    near = toeplitz_tree(taps[1:half], DEPTH - 1)
+    far = toeplitz_tree(taps[half + 1 :], DEPTH - 1)
+    return taps, near, toeplitz_tree(taps[1:], DEPTH), far
+
+
+def added(first, second):
+    return [a + b for a, b in zip(first, second)]
+
+
+def lower(taps, near, x):
+    quarter = TAPS // 4
+    inner = toeplitz(near, x[:quarter])
+    first, second = (
+        [weighted((taps[s - j], part[j]) for j in range(s + 1)) for s in range(quarter)]
+        for part in (x[:quarter], x[quarter:])
+    )
+    return first + added(inner, second)
+
+
+def upper(taps, far, x):
+    quarter = TAPS // 4
+    inner = toeplitz(far, x[quarter:])
+    first, second = (
+        [weighted((taps[TAPS + s - j], part[j]) for j in range(s + 1, quarter)) for s in range(quarter - 1)]
+        for part in (x[:quarter], x[quarter:])
+    )
+    return added(inner, first) + inner[quarter - 1 :] + second
 
 
 def later_frames(tree, x):
-    taps, middle = tree
+    taps, near, middle, far = tree
     half = TAPS // 2
     inner = toeplitz(middle, x[half:])
-    first = [weighted((taps[TAPS + s - j], x[j]) for j in range(s + 1, half)) for s in range(half - 1)]
-    second = [weighted((taps[TAPS + s - j], x[j + half]) for j in range(s + 1, half)) for s in range(half - 1)]
-    return [a + b for a, b in zip(inner, first)] + [inner[half - 1]] + second
+    return added(inner, upper(taps, far, x[:half])) + inner[half - 1 :] + upper(taps, far, x[half:])
 
 
 def these_frames(tree, x):
-    taps, middle = tree
+    taps, near, middle, far = tree
     half = TAPS // 2
     inner = toeplitz(middle, x[:half])
-    first = [weighted((taps[s - j], x[j]) for j in range(s + 1)) for s in range(half)]
-    second = [weighted((taps[s - j], x[j + half]) for j in range(s + 1)) for s in range(half)]
-    return first + [a + b for a, b in zip(second, inner)]
-
-
-def channelize(carried, frames, inputs, x_ref, h_first, h_second, table_ref, out_ref, acc_ref, small_ref):
+    return lower(taps, near, x[:half]) + added(inner, lower(taps, near, x[half:]))
+
+
+def channelize(carried, frames, inputs, x_ref, h_first, h_second, *refs):
     h_refs = h_first, h_second
     step = pl.program_id(0)
     groups = inputs // GROUP
-    turn = lambda start, part, parity: table_ref[pl.ds(start + 2 * part + parity, 1), :]
+    if carried:
+        twiddle_ref, out_ref, table_ref, small_ref = refs
+        turn = lambda start, part, parity: twiddle_ref[pl.ds(start + 2 * part + parity, 1), :]
+    else:
+        table_ref, out_ref = refs
 
     @pl.when(step == 0)
     def _():
-        acc_ref[...] = jnp.zeros_like(acc_ref)
+        out_ref[...] = jnp.zeros_like(out_ref)
+        if not carried:
+            return
         for parity in range(2):
-            real, imag = (table_ref[(2 * part + parity) * FINE : (2 * part + parity + 1) * FINE] for part in range(2))
+            starts = [(2 * part + parity) * FINE for part in range(2)]
+            real, imag = (twiddle_ref[start : start + FINE] for start in starts)
             for k in range(CHUNK // FINE):
                 at = slice(k * FINE, (k + 1) * FINE)
                 turn_real, turn_imag = (turn(4 * FINE + 4 * k, part, parity) for part in range(2))
                 small_ref[0, parity, at] = real * turn_real + imag * turn_imag
                 small_ref[1, parity, at] = imag * turn_real - real * turn_imag
 
-    lines = [[], []]
+    lines = []
     trees = []
     for block in range(CHUNK // LANES):
         lanes = slice(block * LANES, (block + 1) * LANES)
@@ -129,44 +153,51 @@
         for h_ref in h_refs:
             taps = [jnp.broadcast_to(h_ref[t : t + 1, lanes], (GROUP, LANES)) for t in range(TAPS)]
             trees[-1].append(coefficient_tree(taps))
-    for group in range(groups):
-        columns = [[], []]
-        for block in range(CHUNK // LANES):
-            first, second = (
-                (later_frames if carried else these_frames)(
-                    trees[block][part], [x_ref[group, s, part, block].astype(F32) for s in range(frames)]
+    width = TILE // LANES
+    for tile in range(CHUNK // TILE):
+        lines.append([[], []])
+        for group in range(groups):
+            columns = [[], []]
+            for block in range(tile * width, (tile + 1) * width):
+                first, second = (
+                    (later_frames if carried else these_frames)(
+                        trees[block][part], [x_ref[group, s, part, block].astype(F32) for s in range(frames)]
+                    )
+                    for part in range(2)
                 )
-                for part in range(2)
+                for parity in range(2):
+                    values = [a - b if parity else a + b for a, b in zip(first, second)]
+                    if carried:
+                        values.append(jnp.zeros((GROUP, LANES), F32))
+                    pieces = [split(jnp.concatenate(values[s : s + 2], axis=0)) for s in range(0, frames, 2)]
+                    columns[parity].append([jnp.concatenate(part, axis=0) for part in zip(*pieces)])
+            for parity in range(2):
+                lines[tile][parity].append([jnp.concatenate(part, axis=1) for part in zip(*columns[parity])])
+
+    rows = frames * GROUP
+    here = pl.ds(pl.multiple_of(step * CHUNK, CHUNK), CHUNK)
+    for parity in range(2):
+        if carried:
+            start = 4 * FINE + 4 * (CHUNK // FINE) + 4 * step
+            wave = small_ref[0, parity] * turn(start, 0, parity) + small_ref[1, parity] * turn(start, 1, parity)
+            table = jnp.concatenate(split(wave), axis=1)
+            table_ref[parity, here] = table
+        else:
+            table = table_ref[parity, here]
+        total = None
+        for tile in range(CHUNK // TILE):
+            line = lines[tile][parity]
+            order = [line[first + k][part] for first in range(0, groups, SPAN) for part in range(2) for k in range(SPAN)]
+            product = jnp.dot(
+                jnp.concatenate(order, axis=0),
+                table[tile * TILE : (tile + 1) * TILE],
+                preferred_element_type=F32,
             )
-            for parity in range(2):
-                values = [a - b if parity else a + b for a, b in zip(first, second)]
-                if carried:
-                    values.append(jnp.zeros((GROUP, LANES), F32))
-                pieces = [split(jnp.concatenate(values[s : s + 2], axis=0)) for s in range(0, frames, 2)]
-                columns[parity].append(
-                    jnp.concatenate([p[0] for p in pieces] + [p[1] for p in pieces], axis=0)
-                )
-        for parity in range(2):
-            lines[parity].append(jnp.concatenate(columns[parity], axis=1))
-
-    for parity in range(2):
-        start = 4 * FINE + 4 * (CHUNK // FINE) + 4 * step
-        table = small_ref[0, parity] * turn(start, 0, parity) + small_ref[1, parity] * turn(start, 1, parity)
-        total = jnp.dot(
-            jnp.concatenate(lines[parity], axis=0),
-            jnp.concatenate(split(table), axis=1),
-            preferred_element_type=F32,
-        )
-        rows = frames * GROUP
+            total = product if total is None else total + product
         for group in range(groups):
-            high = total[2 * group * rows : (2 * group + 1) * rows]
-            low = total[(2 * group + 1) * rows : (2 * group + 2) * rows]
-            acc_ref[parity, group * rows : (group + 1) * rows] += high + low
-
-    @pl.when(step == pl.num_programs(0) - 1)
-    def _():
-        for parity in range(2):
-            out_ref[parity] = acc_ref[parity, :, :CH] + acc_ref[parity, :, CH:]
+            place = 2 * (group // SPAN) * SPAN + group % SPAN
+            both = total[place * rows : (place + 1) * rows] + total[(place + SPAN) * rows : (place + SPAN + 1) * rows]
+            out_ref[parity, group * rows : (group + 1) * rows] += both[:, :CH] + both[:, CH:]
 
 
 def assemble(frames, inputs, here_ref, before_ref, out_ref):
@@ -196,33 +227,48 @@
     )(here, before).reshape(CH, frames, 2 * inputs)
 
 
-def spectra(voltages, coefficients, carried):
+def spectra(voltages, coefficients, table=None):
     inputs, samples = voltages.shape
     frames = samples // NFFT
-    table, coefficients = (pltpu.with_memory_space_constraint(part, pltpu.HBM) for part in (twiddles(), coefficients))
     steps = HALF // CHUNK
     rows = frames * inputs
+    coefficients = pltpu.with_memory_space_constraint(coefficients, pltpu.HBM)
     tiles = voltages.reshape(inputs // GROUP, GROUP, samples // LANES, LANES).transpose(0, 2, 1, 3)
     tiles = tiles.reshape(inputs // GROUP, frames, 2, HALF // LANES, GROUP, LANES)
     block = (inputs // GROUP, frames, 2, CHUNK // LANES, GROUP, LANES)
-    return pl.pallas_call(
-        functools.partial(channelize, carried, frames, inputs),
-        out_shape=jax.ShapeDtypeStruct((2, rows, CH), F32),
+    in_specs = [
+        pl.BlockSpec(block, lambda j: (0, 0, 0, j, 0, 0)),
+        pl.BlockSpec((TAPS, CHUNK), lambda j: (0, j)),
+        pl.BlockSpec((TAPS, CHUNK), lambda j: (0, steps + j)),
+    ]
+    out_shape = jax.ShapeDtypeStruct((2, rows, CH), F32)
+    whole = pl.BlockSpec(memory_space=pltpu.VMEM)
+    options = dict(
         grid=(steps,),
-        in_specs=[
-            pl.BlockSpec(block, lambda j: (0, 0, 0, j, 0, 0)),
-            pl.BlockSpec((TAPS, CHUNK), lambda j: (0, j)),
-            pl.BlockSpec((TAPS, CHUNK), lambda j: (0, steps + j)),
-            pl.BlockSpec(table.shape, lambda j: (0, 0)),
-        ],
-        out_specs=pl.BlockSpec((2, rows, CH), lambda j: (0, 0, 0)),
-        scratch_shapes=[pltpu.VMEM((2, rows, 2 * CH), F32), pltpu.VMEM((2, 2, CHUNK, CH), F32)],
         compiler_params=pltpu.CompilerParams(vmem_limit_bytes=48 * 2**20),
         cost_estimate=pl.CostEstimate(
             flops=4 * rows * NFFT * 2 * CH, bytes_accessed=2 * inputs * samples, transcendentals=0
         ),
-        name="carried" if carried else "current",
-    )(tiles, coefficients, coefficients, table)
+    )
+    if table is not None:
+        return pl.pallas_call(
+            functools.partial(channelize, False, frames, inputs),
+            out_shape=out_shape,
+            in_specs=in_specs + [whole],
+            out_specs=whole,
+            name="current",
+            **options,
+        )(tiles, coefficients, coefficients, table)
+    waves = pltpu.with_memory_space_constraint(twiddles(), pltpu.HBM)
+    return pl.pallas_call(
+        functools.partial(channelize, True, frames, inputs),
+        out_shape=(out_shape, jax.ShapeDtypeStruct((2, HALF, 2 * CH), BF16)),
+        in_specs=in_specs + [pl.BlockSpec(waves.shape, lambda j: (0, 0))],
+        out_specs=(whole, whole),
+        scratch_shapes=[pltpu.VMEM((2, 2, CHUNK, CH), F32)],
+        name="carried",
+        **options,
+    )(tiles, coefficients, coefficients, waves)
 
 
 def correlate(n_time, n_input, inputs, frames, got_ref, out_ref, left_high, left_low, right_high, right_low):
@@ -265,12 +311,12 @@
     inputs = width // 2
     total = n_input * inputs
     depth = 2 * n_time * frames
-    block = 128
+    block = 256
     return pl.pallas_call(
         functools.partial(correlate, n_time, n_input, inputs, frames),
         out_shape=jax.ShapeDtypeStruct((2, 1, total, total), F32),
         grid=(total // block,),
-        in_specs=[pl.BlockSpec(received.shape, lambda j: (0, 0, 0))],
+        in_specs=[pl.BlockSpec(memory_space=pltpu.VMEM)],
         out_specs=pl.BlockSpec((2, 1, block, total), lambda j: (0, 0, j, 0)),
         scratch_shapes=[pltpu.VMEM((total, depth), BF16)] * 2 + [pltpu.VMEM((2, depth, total), BF16)] * 2,
         compiler_params=pltpu.CompilerParams(vmem_limit_bytes=48 * 2**20),
@@ -281,9 +327,9 @@
 def shards(voltages, coefficients):
     n_time = lax.axis_size("tm")
     n_input = lax.axis_size("inp")
-    carried = spectra(voltages, coefficients, True)
+    carried, table = spectra(voltages, coefficients)
     arrived = lax.ppermute(carried, "tm", [(i, i + 1) for i in range(n_time - 1)])
-    current = spectra(voltages, coefficients, False)
+    current = spectra(voltages, coefficients, table)
     outgoing = messages(current, arrived, voltages.shape[0])
     received = lax.all_to_all(outgoing, ("tm", "inp"), split_axis=0, concat_axis=0, tiled=True)
     return visibilities(received, n_time, n_input)

time: 96.8 us -> 93.8 us (0.969)
  Pallas kernels: 63 us -> 59.8 us
    pallas_call x2, Pallas kernels: 54.3 us -> 52.4 us  [the longest x1 26.5 us: spectra(): pl.pallas_call(functools.partial(channelize, False, frames, inputs), out_...]
    pallas_call x1, Pallas kernels: 7.53 us -> 6.29 us  [visibilities(): pl.pallas_call(functools.partial(correlate, n_time, n_input, inputs, fram...]
  transfers between devices with their start and end apart: 1 -> 1, of which waited for: 0 -> 0; matrix products, arithmetic and copies ran while one was open for 0% -> 0% of each run, Pallas kernels for 30% -> 28%
where the time goes in v3:
time: 93.8 us; the launch traced here: 93.6 us
  Pallas kernels  59.8 us (64%)
  blocking collectives  29.7 us (32%)
  starting transfers between devices  4 us (4%)
    all_to_all x1, blocking collectives, shards(): lax.all_to_all(outgoing, ('tm', 'inp'), split_axis=0, concat_axis=0, tile...  29.7 us
    pallas_call x1, Pallas kernels, spectra(): pl.pallas_call(functools.partial(channelize, False, frames, inputs), out_...  26.5 us
    pallas_call x1, Pallas kernels, spectra(): pl.pallas_call(functools.partial(channelize, True, frames, inputs), out_s...  25.9 us
    pallas_call x1, Pallas kernels, visibilities(): pl.pallas_call(functools.partial(correlate, n_time, n_input, inputs, fram...  6.29 us
    ppermute x1, starting transfers between devices, shards(): lax.ppermute(carried, 'tm', [(i, i + 1) for i in range(n_time - 1)])  4 us
  transfers between devices with their start and end apart: 1, of which 0 were waited for; matrix products, arithmetic and copies ran while one was open for 0% of the time, Pallas kernels for 28%

profile of v3, /device:TPU:1, one launch (start us, length us, event | category | flops | bytes accessed | tf_op | source)
XLA Modules:
  0.0 93.6 jit_solution(12071139997242145155)
XLA Ops:
  0.0 25.9 %carried.1 = (f32[2,1024,128]{2,1,0:T(8,128)S(1)}, bf16[2,4096,256]{2,1,0:T(8,128)(2,1)S(1)}) custom-call(bf16[8,16,2,32,8,128]{5,4,3,2,1,0:T(8,128)(2,1)} %bitcast.7, f32[16,8192]{1,0:T(8,128)} %h_second.3, f32[16,8192]{1,0:T(8,128)} %h_second.3, f32[224,128]{1,0:T(8,128)} %constant.2.clone.refs_0_), custom_call_target="tpu_custom_call" | custom-call | flops 8589934592 | bytes 16777216 | tf_op jit(solution)/shard_map/carried/pallas_call | solution.py:263
  26.0 4.0 %collective-permute-start = (f32[2,1024,128]{2,1,0:T(8,128)S(1)}, f32[2,1024,128]{2,1,0:T(8,128)S(1)}, u32[]{:S(2)}, u32[]{:S(2)}) collective-permute-start(f32[2,1024,128]{2,1,0:T(8,128)S(1)} %get-tuple-element.8), channel_id=1, source_target_pairs={{0,16},{16,32},{32,48},{48,64},{64,80},{80,96},{96,112},{1,17},{17... | collective-permute-start | bytes 3145736 | tf_op jit(solution)/shard_map/ppermute | solution.py:331
  30.0 26.5 %current.1.here_ref = f32[2,1024,128]{2,1,0:T(8,128)S(1)} custom-call(bf16[8,16,2,32,8,128]{5,4,3,2,1,0:T(8,128)(2,1)} %bitcast.8, f32[16,8192]{1,0:T(8,128)} %h_second.3, f32[16,8192]{1,0:T(8,128)} %h_second.3, bf16[2,4096,256]{2,1,0:T(8,128)(2,1)S(1)} %get-tuple-element.7.refs_0_), custom_call_target="tpu_custom_call" | custom-call | flops 8589934592 | bytes 16777216 | tf_op jit(solution)/shard_map/current/pallas_call | solution.py:254
  56.5 0.0 collective-permute-done.before_ref
  56.5 1.1 %messages.1 = f32[64,2,16,128]{3,2,1,0:T(8,128)S(1)} custom-call(f32[2,1024,128]{2,1,0:T(8,128)S(1)} %current.1.here_ref, f32[2,1024,128]{2,1,0:T(8,128)S(1)} %collective-permute-done.before_ref), custom_call_target="tpu_custom_call" | custom-call | tf_op jit(solution)/shard_map/messages/pallas_call | solution.py:222
  57.6 29.7 %all_to_all.5.got_ref = f32[128,16,128]{2,1,0:T(8,128)S(1)} all-to-all(f32[128,16,128]{2,1,0:T(8,128)S(1)} %bitcast.6), channel_id=1, replica_groups=mesh['tm'=8,'inp'=16] {'tm','inp'}, dimensions={0} | all-to-all | bytes 2097152 | tf_op jit(solution)/shard_map/all_to_all | solution.py:334
  87.3 6.3 %correlate.1 = f32[2,1,1024,1024]{3,2,1,0:T(8,128)} custom-call(f32[128,16,128]{2,1,0:T(8,128)S(1)} %all_to_all.5.got_ref), custom_call_target="tpu_custom_call" | custom-call | tf_op jit(solution)/shard_map/correlate/pallas_call | solution.py:315
Async XLA Ops:
  26.0 30.5 %collective-permute-start = (f32[2,1024,128]{2,1,0:T(8,128)S(1)}, f32[2,1024,128]{2,1,0:T(8,128)S(1)}, u32[]{:S(2)}, u32[]{:S(2)}) collective-permute-start(f32[2,1024,128]{2,1,0:T(8,128)S(1)} %get-tuple-element.8), channel_id=1, source_target_pairs={{0,16},{16,32},{32,48},{48,64},{64,80},{80,96},{96,112},{1,17},{17... | collective-permute-start | bytes 3145736 | tf_op jit(solution)/shard_map/ppermute | solution.py:331

commit v4 on v3

--- a/solution.py
+++ b/solution.py
@@ -19,6 +19,7 @@
 FINE = 16
 TILE = 512
 SPAN = 8
+BATCH = 1
 DEPTH = 2
 F32 = jnp.float32
 BF16 = jnp.bfloat16
@@ -121,15 +122,58 @@
     return lower(taps, near, x[:half]) + added(inner, lower(taps, near, x[half:]))
 
 
-def channelize(carried, frames, inputs, x_ref, h_first, h_second, *refs):
-    h_refs = h_first, h_second
+def ahead_copies(tiles_ref, coefficients_ref, ahead_ref, taps_ref, sems):
+    width = CHUNK // LANES
+    return [
+        pltpu.make_async_copy(tiles_ref.at[:, :, :, pl.ds(0, width)], ahead_ref.at[0], sems.at[0]),
+        pltpu.make_async_copy(coefficients_ref, taps_ref, sems.at[1]),
+    ]
+
+
+def block_copy(tiles_ref, ahead_ref, sems, step):
+    width = CHUNK // LANES
+    source = tiles_ref.at[:, :, :, pl.ds(step * width, width)]
+    slot = lax.rem(step, 2)
+    return pltpu.make_async_copy(source, ahead_ref.at[slot], sems.at[slot])
+
+
+def channelize(carried, frames, inputs, *refs):
     step = pl.program_id(0)
+    steps = HALF // CHUNK
     groups = inputs // GROUP
     if carried:
-        twiddle_ref, out_ref, table_ref, small_ref = refs
+        x_ref, h_first, h_second, twiddle_ref, tiles_ref, coefficients_ref = refs[:6]
+        out_ref, table_ref, ahead_ref, taps_ref, small_ref, sems = refs[6:]
         turn = lambda start, part, parity: twiddle_ref[pl.ds(start + 2 * part + parity, 1), :]
+        sample = lambda group, s, part, block: x_ref[group, s, part, block]
+        tap = lambda t, part, block: (h_first, h_second)[part][t : t + 1, block * LANES : (block + 1) * LANES]
+        copies = ahead_copies(tiles_ref, coefficients_ref, ahead_ref, taps_ref, sems)
+
+        @pl.when(step == 0)
+        def _():
+            for copy in copies:
+                copy.start()
+
+        @pl.when(step == steps - 1)
+        def _():
+            for copy in copies:
+                copy.wait()
     else:
-        table_ref, out_ref = refs
+        tiles_ref, h_ref, table_ref, _, out_ref, ahead_ref, sems = refs
+        slot = lax.rem(step, 2)
+        sample = lambda group, s, part, block: ahead_ref[slot, group, s, part, block]
+
+        def tap(t, part, block):
+            start = pl.multiple_of(part * HALF + step * CHUNK + block * LANES, LANES)
+            return h_ref[t : t + 1, pl.ds(start, LANES)]
+
+        @pl.when(step > 0)
+        def _():
+            block_copy(tiles_ref, ahead_ref, sems, step).wait()
+
+        @pl.when(step + 1 < steps)
+        def _():
+            block_copy(tiles_ref, ahead_ref, sems, step + 1).start()
 
     @pl.when(step == 0)
     def _():
@@ -148,31 +192,36 @@
     lines = []
     trees = []
     for block in range(CHUNK // LANES):
-        lanes = slice(block * LANES, (block + 1) * LANES)
         trees.append([])
-        for h_ref in h_refs:
-            taps = [jnp.broadcast_to(h_ref[t : t + 1, lanes], (GROUP, LANES)) for t in range(TAPS)]
+        for part in range(2):
+            taps = [jnp.broadcast_to(tap(t, part, block), (GROUP, LANES)) for t in range(TAPS)]
             trees[-1].append(coefficient_tree(taps))
     width = TILE // LANES
     for tile in range(CHUNK // TILE):
         lines.append([[], []])
-        for group in range(groups):
-            columns = [[], []]
+        for start in range(0, groups, BATCH):
+            batch = range(start, start + BATCH)
+            columns = [[[], []] for _ in batch]
             for block in range(tile * width, (tile + 1) * width):
                 first, second = (
-                    (later_frames if carried else these_frames)(
-                        trees[block][part], [x_ref[group, s, part, block].astype(F32) for s in range(frames)]
-                    )
+                    [
+                        (later_frames if carried else these_frames)(
+                            trees[block][part], [sample(group, s, part, block).astype(F32) for s in range(frames)]
+                        )
+                        for group in batch
+                    ]
                     for part in range(2)
                 )
+                for column, one, other in zip(columns, first, second):
+                    for parity in range(2):
+                        values = [a - b if parity else a + b for a, b in zip(one, other)]
+                        if carried:
+                            values.append(jnp.zeros((GROUP, LANES), F32))
+                        pieces = [split(jnp.concatenate(values[s : s + 2], axis=0)) for s in range(0, frames, 2)]
+                        column[parity].append([jnp.concatenate(part, axis=0) for part in zip(*pieces)])
+            for column in columns:
                 for parity in range(2):
-                    values = [a - b if parity else a + b for a, b in zip(first, second)]
-                    if carried:
-                        values.append(jnp.zeros((GROUP, LANES), F32))
-                    pieces = [split(jnp.concatenate(values[s : s + 2], axis=0)) for s in range(0, frames, 2)]
-                    columns[parity].append([jnp.concatenate(part, axis=0) for part in zip(*pieces)])
-            for parity in range(2):
-                lines[tile][parity].append([jnp.concatenate(part, axis=1) for part in zip(*columns[parity])])
+                    lines[tile][parity].append([jnp.concatenate(part, axis=1) for part in zip(*column[parity])])
 
     rows = frames * GROUP
     here = pl.ds(pl.multiple_of(step * CHUNK, CHUNK), CHUNK)
@@ -227,48 +276,64 @@
     )(here, before).reshape(CH, frames, 2 * inputs)
 
 
-def spectra(voltages, coefficients, table=None):
-    inputs, samples = voltages.shape
-    frames = samples // NFFT
-    steps = HALF // CHUNK
-    rows = frames * inputs
-    coefficients = pltpu.with_memory_space_constraint(coefficients, pltpu.HBM)
-    tiles = voltages.reshape(inputs // GROUP, GROUP, samples // LANES, LANES).transpose(0, 2, 1, 3)
-    tiles = tiles.reshape(inputs // GROUP, frames, 2, HALF // LANES, GROUP, LANES)
-    block = (inputs // GROUP, frames, 2, CHUNK // LANES, GROUP, LANES)
-    in_specs = [
-        pl.BlockSpec(block, lambda j: (0, 0, 0, j, 0, 0)),
-        pl.BlockSpec((TAPS, CHUNK), lambda j: (0, j)),
-        pl.BlockSpec((TAPS, CHUNK), lambda j: (0, steps + j)),
-    ]
-    out_shape = jax.ShapeDtypeStruct((2, rows, CH), F32)
-    whole = pl.BlockSpec(memory_space=pltpu.VMEM)
-    options = dict(
-        grid=(steps,),
-        compiler_params=pltpu.CompilerParams(vmem_limit_bytes=48 * 2**20),
+def options(inputs, samples):
+    rows = samples // NFFT * inputs
+    return dict(
+        grid=(HALF // CHUNK,),
+        compiler_params=pltpu.CompilerParams(vmem_limit_bytes=40 * 2**20),
         cost_estimate=pl.CostEstimate(
             flops=4 * rows * NFFT * 2 * CH, bytes_accessed=2 * inputs * samples, transcendentals=0
         ),
     )
-    if table is not None:
+
+
+def spectra(voltages, coefficients):
+    inputs, samples = voltages.shape
+    frames = samples // NFFT
+    steps = HALF // CHUNK
+    whole, anywhere = pl.BlockSpec(memory_space=pltpu.VMEM), pl.BlockSpec(memory_space=pl.ANY)
+    coefficients = pltpu.with_memory_space_constraint(coefficients, pltpu.HBM)
+    waves = pltpu.with_memory_space_constraint(twiddles(), pltpu.HBM)
+    tiles = voltages.reshape(inputs // GROUP, GROUP, samples // LANES, LANES).transpose(0, 2, 1, 3)
+    tiles = tiles.reshape(inputs // GROUP, frames, 2, HALF // LANES, GROUP, LANES)
+    block = (inputs // GROUP, frames, 2, CHUNK // LANES, GROUP, LANES)
+    sums = jax.ShapeDtypeStruct((2, frames * inputs, CH), F32)
+    ahead = jax.ShapeDtypeStruct((2,) + block, BF16)
+    carried, table, ahead, taps = pl.pallas_call(
+        functools.partial(channelize, True, frames, inputs),
+        out_shape=(
+            sums,
+            jax.ShapeDtypeStruct((2, HALF, 2 * CH), BF16),
+            ahead,
+            jax.ShapeDtypeStruct(coefficients.shape, F32),
+        ),
+        in_specs=[
+            pl.BlockSpec(block, lambda j: (0, 0, 0, j, 0, 0)),
+            pl.BlockSpec((TAPS, CHUNK), lambda j: (0, j)),
+            pl.BlockSpec((TAPS, CHUNK), lambda j: (0, steps + j)),
+            pl.BlockSpec(waves.shape, lambda j: (0, 0)),
+            anywhere,
+            anywhere,
+        ],
+        out_specs=(whole,) * 4,
+        scratch_shapes=[pltpu.VMEM((2, 2, CHUNK, CH), F32), pltpu.SemaphoreType.DMA((2,))],
+        name="carried",
+        **options(inputs, samples),
+    )(tiles, coefficients, coefficients, waves, tiles, coefficients)
+
+    def current():
         return pl.pallas_call(
             functools.partial(channelize, False, frames, inputs),
-            out_shape=out_shape,
-            in_specs=in_specs + [whole],
-            out_specs=whole,
+            out_shape=(sums, jax.ShapeDtypeStruct(ahead.shape, BF16)),
+            in_specs=[anywhere, whole, whole, whole],
+            out_specs=(whole, whole),
+            scratch_shapes=[pltpu.SemaphoreType.DMA((2,))],
+            input_output_aliases={3: 1},
             name="current",
-            **options,
-        )(tiles, coefficients, coefficients, table)
-    waves = pltpu.with_memory_space_constraint(twiddles(), pltpu.HBM)
-    return pl.pallas_call(
-        functools.partial(channelize, True, frames, inputs),
-        out_shape=(out_shape, jax.ShapeDtypeStruct((2, HALF, 2 * CH), BF16)),
-        in_specs=in_specs + [pl.BlockSpec(waves.shape, lambda j: (0, 0))],
-        out_specs=(whole, whole),
-        scratch_shapes=[pltpu.VMEM((2, 2, CHUNK, CH), F32)],
-        name="carried",
-        **options,
-    )(tiles, coefficients, coefficients, waves)
+            **options(inputs, samples),
+        )(tiles, taps, table, ahead)[0]
+
+    return carried, current
 
 
 def correlate(n_time, n_input, inputs, frames, got_ref, out_ref, left_high, left_low, right_high, right_low):
@@ -327,10 +392,9 @@
 def shards(voltages, coefficients):
     n_time = lax.axis_size("tm")
     n_input = lax.axis_size("inp")
-    carried, table = spectra(voltages, coefficients)
+    carried, current = spectra(voltages, coefficients)
     arrived = lax.ppermute(carried, "tm", [(i, i + 1) for i in range(n_time - 1)])
-    current = spectra(voltages, coefficients, table)
-    outgoing = messages(current, arrived, voltages.shape[0])
+    outgoing = messages(current(), arrived, voltages.shape[0])
     received = lax.all_to_all(outgoing, ("tm", "inp"), split_axis=0, concat_axis=0, tiled=True)
     return visibilities(received, n_time, n_input)
 

time: 93.8 us -> 92.6 us (0.987)
  Pallas kernels: 59.8 us -> 58.8 us
    pallas_call x1, Pallas kernels: 26.5 us -> 25.4 us  [current(): pl.pallas_call(functools.partial(channelize, False, frames, inputs), out_...]
  transfers between devices with their start and end apart: 1 -> 1, of which waited for: 0 -> 0; matrix products, arithmetic and copies ran while one was open for 0% -> 0% of each run, Pallas kernels for 28% -> 27%
where the time goes in v4:
time: 92.6 us; the launch traced here: 92.4 us
  Pallas kernels  58.8 us (63%)
  blocking collectives  29.6 us (32%)
  starting transfers between devices  4 us (4%)
    all_to_all x1, blocking collectives, shards(): lax.all_to_all(outgoing, ('tm', 'inp'), split_axis=0, concat_axis=0, tile...  29.6 us
    pallas_call x1, Pallas kernels, spectra(): pl.pallas_call(functools.partial(channelize, True, frames, inputs), out_s...  26 us
    pallas_call x1, Pallas kernels, current(): pl.pallas_call(functools.partial(channelize, False, frames, inputs), out_...  25.4 us
    pallas_call x1, Pallas kernels, visibilities(): pl.pallas_call(functools.partial(correlate, n_time, n_input, inputs, fram...  6.29 us
    ppermute x1, starting transfers between devices, shards(): lax.ppermute(carried, 'tm', [(i, i + 1) for i in range(n_time - 1)])  4 us
  transfers between devices with their start and end apart: 1, of which 0 were waited for; matrix products, arithmetic and copies ran while one was open for 0% of the time, Pallas kernels for 27%

profile of v4, /device:TPU:1, one launch (start us, length us, event | category | flops | bytes accessed | tf_op | source)
XLA Modules:
  0.0 92.4 jit_solution(15222737679956905421)
XLA Ops:
  0.0 26.0 %carried.1 = (f32[2,1024,128]{2,1,0:T(8,128)S(1)}, bf16[2,4096,256]{2,1,0:T(8,128)(2,1)S(1)}, bf16[2,8,16,2,4,8,128]{6,5,4,3,2,1,0:T(8,128)(2,1)S(1)}, f32[16,8192]{1,0:T(8,128)S(1)}) custom-call(bf16[8,16,2,32,8,128]{5,4,3,2,1,0:T(8,128)(2,1)} %bitcast.7, f32[16,8192]{1,0:T(8,128)} %refs_5_.1, f32[16,8192]{1,0:T(8,128)} %refs_5_.1, ...), custom_call_target="tpu_custom_call" | custom-call | flops 8589934592 | bytes 16777216 | tf_op jit(solution)/shard_map/carried/pallas_call | solution.py:302
  26.0 4.0 %collective-permute-start = (f32[2,1024,128]{2,1,0:T(8,128)S(1)}, f32[2,1024,128]{2,1,0:T(8,128)S(1)}, u32[]{:S(2)}, u32[]{:S(2)}) collective-permute-start(f32[2,1024,128]{2,1,0:T(8,128)S(1)} %get-tuple-element.14), channel_id=1, source_target_pairs={{0,16},{16,32},{32,48},{48,64},{64,80},{80,96},{96,112},{1,17},{17... | collective-permute-start | bytes 3145736 | tf_op jit(solution)/shard_map/ppermute | solution.py:396
  30.0 25.4 %current.1 = (f32[2,1024,128]{2,1,0:T(8,128)S(1)}, bf16[2,8,16,2,4,8,128]{6,5,4,3,2,1,0:T(8,128)(2,1)S(1)}) custom-call(bf16[8,16,2,32,8,128]{5,4,3,2,1,0:T(8,128)(2,1)} %bitcast.9, f32[16,8192]{1,0:T(8,128)S(1)} %get-tuple-element.10.refs_1_, bf16[2,4096,256]{2,1,0:T(8,128)(2,1)S(1)} %get-tuple-element.11.refs_2_, ...), custom_call_target="tpu_custom_call", output_to_operand_aliasing={{1}: (3, {})} | custom-call | flops 8589934592 | bytes 16777216 | tf_op jit(solution)/shard_map/current/pallas_call | solution.py:325
  55.4 0.0 collective-permute-done.before_ref
  55.4 1.1 %messages.1 = f32[64,2,16,128]{3,2,1,0:T(8,128)S(1)} custom-call(f32[2,1024,128]{2,1,0:T(8,128)S(1)} %get-tuple-element.13.here_ref, f32[2,1024,128]{2,1,0:T(8,128)S(1)} %collective-permute-done.before_ref), custom_call_target="tpu_custom_call" | custom-call | tf_op jit(solution)/shard_map/messages/pallas_call | solution.py:271
  56.5 29.6 %all_to_all.5.got_ref = f32[128,16,128]{2,1,0:T(8,128)S(1)} all-to-all(f32[128,16,128]{2,1,0:T(8,128)S(1)} %bitcast.6), channel_id=1, replica_groups=mesh['tm'=8,'inp'=16] {'tm','inp'}, dimensions={0} | all-to-all | bytes 2097152 | tf_op jit(solution)/shard_map/all_to_all | solution.py:398
  86.2 6.3 %correlate.1 = f32[2,1,1024,1024]{3,2,1,0:T(8,128)} custom-call(f32[128,16,128]{2,1,0:T(8,128)S(1)} %all_to_all.5.got_ref), custom_call_target="tpu_custom_call" | custom-call | tf_op jit(solution)/shard_map/correlate/pallas_call | solution.py:380
Async XLA Ops:
  26.0 29.4 %collective-permute-start = (f32[2,1024,128]{2,1,0:T(8,128)S(1)}, f32[2,1024,128]{2,1,0:T(8,128)S(1)}, u32[]{:S(2)}, u32[]{:S(2)}) collective-permute-start(f32[2,1024,128]{2,1,0:T(8,128)S(1)} %get-tuple-element.14), channel_id=1, source_target_pairs={{0,16},{16,32},{32,48},{48,64},{64,80},{80,96},{96,112},{1,17},{17... | collective-permute-start | bytes 3145736 | tf_op jit(solution)/shard_map/ppermute | solution.py:396

commit v5 on v4

--- a/solution.py
+++ b/solution.py
@@ -13,11 +13,11 @@
 CH = 128
 CH0 = 1024
 LANES = 128
-CHUNK = 512
+CHUNK = 1024
 HALF = NFFT // 2
 GROUP = 8
 FINE = 16
-TILE = 512
+TILE = 1024
 SPAN = 8
 BATCH = 1
 DEPTH = 2

time: 92.6 us -> 91.7 us (level)
  Pallas kernels: 58.8 us -> 57.7 us
where the time goes in v5:
time: 91.7 us; the launch traced here: 91.6 us
  Pallas kernels  57.7 us (63%)
  blocking collectives  29.7 us (32%)
  starting transfers between devices  4.19 us (5%)
    all_to_all x1, blocking collectives, shards(): lax.all_to_all(outgoing, ('tm', 'inp'), split_axis=0, concat_axis=0, tile...  29.7 us
    pallas_call x1, Pallas kernels, spectra(): pl.pallas_call(functools.partial(channelize, True, frames, inputs), out_s...  25.8 us
    pallas_call x1, Pallas kernels, current(): pl.pallas_call(functools.partial(channelize, False, frames, inputs), out_...  24.5 us
    pallas_call x1, Pallas kernels, visibilities(): pl.pallas_call(functools.partial(correlate, n_time, n_input, inputs, fram...  6.29 us
    ppermute x1, starting transfers between devices, shards(): lax.ppermute(carried, 'tm', [(i, i + 1) for i in range(n_time - 1)])  4.19 us
  transfers between devices with their start and end apart: 1, of which 0 were waited for; matrix products, arithmetic and copies ran while one was open for 0% of the time, Pallas kernels for 27%

profile of v5, /device:TPU:1, one launch (start us, length us, event | category | flops | bytes accessed | tf_op | source)
XLA Modules:
  0.0 91.6 jit_solution(5184399310290637786)
XLA Ops:
  0.0 25.8 %carried.1 = (f32[2,1024,128]{2,1,0:T(8,128)S(1)}, bf16[2,4096,256]{2,1,0:T(8,128)(2,1)S(1)}, bf16[2,8,16,2,8,8,128]{6,5,4,3,2,1,0:T(8,128)(2,1)S(1)}, f32[16,8192]{1,0:T(8,128)S(1)}) custom-call(bf16[8,16,2,32,8,128]{5,4,3,2,1,0:T(8,128)(2,1)} %bitcast.7, f32[16,8192]{1,0:T(8,128)} %refs_5_.1, f32[16,8192]{1,0:T(8,128)} %refs_5_.1, ...), custom_call_target="tpu_custom_call" | custom-call | flops 8589934592 | bytes 16777216 | tf_op jit(solution)/shard_map/carried/pallas_call | solution.py:302
  25.8 4.2 %collective-permute-start = (f32[2,1024,128]{2,1,0:T(8,128)S(1)}, f32[2,1024,128]{2,1,0:T(8,128)S(1)}, u32[]{:S(2)}, u32[]{:S(2)}) collective-permute-start(f32[2,1024,128]{2,1,0:T(8,128)S(1)} %get-tuple-element.14), channel_id=1, source_target_pairs={{0,16},{16,32},{32,48},{48,64},{64,80},{80,96},{96,112},{1,17},{17... | collective-permute-start | bytes 3145736 | tf_op jit(solution)/shard_map/ppermute | solution.py:396
  30.0 24.5 %current.1 = (f32[2,1024,128]{2,1,0:T(8,128)S(1)}, bf16[2,8,16,2,8,8,128]{6,5,4,3,2,1,0:T(8,128)(2,1)S(1)}) custom-call(bf16[8,16,2,32,8,128]{5,4,3,2,1,0:T(8,128)(2,1)} %bitcast.9, f32[16,8192]{1,0:T(8,128)S(1)} %get-tuple-element.10.refs_1_, bf16[2,4096,256]{2,1,0:T(8,128)(2,1)S(1)} %get-tuple-element.11.refs_2_, ...), custom_call_target="tpu_custom_call", output_to_operand_aliasing={{1}: (3, {})} | custom-call | flops 8589934592 | bytes 16777216 | tf_op jit(solution)/shard_map/current/pallas_call | solution.py:325
  54.5 0.0 collective-permute-done.before_ref
  54.5 1.1 %messages.1 = f32[64,2,16,128]{3,2,1,0:T(8,128)S(1)} custom-call(f32[2,1024,128]{2,1,0:T(8,128)S(1)} %get-tuple-element.13.here_ref, f32[2,1024,128]{2,1,0:T(8,128)S(1)} %collective-permute-done.before_ref), custom_call_target="tpu_custom_call" | custom-call | tf_op jit(solution)/shard_map/messages/pallas_call | solution.py:271
  55.6 29.7 %all_to_all.5.got_ref = f32[128,16,128]{2,1,0:T(8,128)S(1)} all-to-all(f32[128,16,128]{2,1,0:T(8,128)S(1)} %bitcast.6), channel_id=1, replica_groups=mesh['tm'=8,'inp'=16] {'tm','inp'}, dimensions={0} | all-to-all | bytes 2097152 | tf_op jit(solution)/shard_map/all_to_all | solution.py:398
  85.3 6.3 %correlate.1 = f32[2,1,1024,1024]{3,2,1,0:T(8,128)} custom-call(f32[128,16,128]{2,1,0:T(8,128)S(1)} %all_to_all.5.got_ref), custom_call_target="tpu_custom_call" | custom-call | tf_op jit(solution)/shard_map/correlate/pallas_call | solution.py:380
Async XLA Ops:
  25.8 28.7 %collective-permute-start = (f32[2,1024,128]{2,1,0:T(8,128)S(1)}, f32[2,1024,128]{2,1,0:T(8,128)S(1)}, u32[]{:S(2)}, u32[]{:S(2)}) collective-permute-start(f32[2,1024,128]{2,1,0:T(8,128)S(1)} %get-tuple-element.14), channel_id=1, source_target_pairs={{0,16},{16,32},{32,48},{48,64},{64,80},{80,96},{96,112},{1,17},{17... | collective-permute-start | bytes 3145736 | tf_op jit(solution)/shard_map/ppermute | solution.py:396

commit v6 on v5

--- a/solution.py
+++ b/solution.py
@@ -340,7 +340,9 @@
     count = n_time * frames
     dot = functools.partial(jnp.dot, preferred_element_type=F32)
 
-    @pl.when(pl.program_id(0) == 0)
+    part = pl.program_id(1)
+
+    @pl.when((pl.program_id(0) == 0) & (part == 0))
     def _():
         for i in range(n_time):
             real_rows = slice(i * frames, (i + 1) * frames)
@@ -366,9 +368,8 @@
     size = out_ref.shape[2]
     rows = pl.ds(pl.multiple_of(pl.program_id(0) * size, size), size)
     high, low = left_high[rows, :], left_low[rows, :]
-    for part in range(2):
-        total = dot(high, right_high[part]) + dot(high, right_low[part]) + dot(low, right_high[part])
-        out_ref[part, 0] = total * (1.0 / count)
+    total = dot(high, right_high[part]) + dot(high, right_low[part]) + dot(low, right_high[part])
+    out_ref[0, 0] = total * (1.0 / count)
 
 
 def visibilities(received, n_time, n_input):
@@ -380,9 +381,9 @@
     return pl.pallas_call(
         functools.partial(correlate, n_time, n_input, inputs, frames),
         out_shape=jax.ShapeDtypeStruct((2, 1, total, total), F32),
-        grid=(total // block,),
+        grid=(total // block, 2),
         in_specs=[pl.BlockSpec(memory_space=pltpu.VMEM)],
-        out_specs=pl.BlockSpec((2, 1, block, total), lambda j: (0, 0, j, 0)),
+        out_specs=pl.BlockSpec((1, 1, block, total), lambda j, part: (part, 0, j, 0)),
         scratch_shapes=[pltpu.VMEM((total, depth), BF16)] * 2 + [pltpu.VMEM((2, depth, total), BF16)] * 2,
         compiler_params=pltpu.CompilerParams(vmem_limit_bytes=48 * 2**20),
         name="correlate",

time: 91.7 us -> 92.9 us (1.013)
  Pallas kernels: 57.7 us -> 58.8 us
    pallas_call x1, Pallas kernels: 6.29 us -> 7.46 us  [visibilities(): pl.pallas_call(functools.partial(correlate, n_time, n_input, inputs, fram...]
  transfers between devices with their start and end apart: 1 -> 1, of which waited for: 0 -> 0; matrix products, arithmetic and copies ran while one was open for 0% -> 0% of each run, Pallas kernels for 27% -> 26%
where the time goes in v6:
time: 92.9 us; the launch traced here: 92.7 us
  Pallas kernels  58.8 us (63%)
  blocking collectives  29.7 us (32%)
  starting transfers between devices  4.19 us (5%)
    all_to_all x1, blocking collectives, shards(): lax.all_to_all(outgoing, ('tm', 'inp'), split_axis=0, concat_axis=0, tile...  29.7 us
    pallas_call x1, Pallas kernels, spectra(): pl.pallas_call(functools.partial(channelize, True, frames, inputs), out_s...  25.8 us
    pallas_call x1, Pallas kernels, current(): pl.pallas_call(functools.partial(channelize, False, frames, inputs), out_...  24.5 us
    pallas_call x1, Pallas kernels, visibilities(): pl.pallas_call(functools.partial(correlate, n_time, n_input, inputs, fram...  7.46 us
    ppermute x1, starting transfers between devices, shards(): lax.ppermute(carried, 'tm', [(i, i + 1) for i in range(n_time - 1)])  4.19 us
  transfers between devices with their start and end apart: 1, of which 0 were waited for; matrix products, arithmetic and copies ran while one was open for 0% of the time, Pallas kernels for 26%

profile of v6, /device:TPU:1, one launch (start us, length us, event | category | flops | bytes accessed | tf_op | source)
XLA Modules:
  0.0 92.7 jit_solution(693532299154616236)
XLA Ops:
  0.0 25.8 %carried.1 = (f32[2,1024,128]{2,1,0:T(8,128)S(1)}, bf16[2,4096,256]{2,1,0:T(8,128)(2,1)S(1)}, bf16[2,8,16,2,8,8,128]{6,5,4,3,2,1,0:T(8,128)(2,1)S(1)}, f32[16,8192]{1,0:T(8,128)S(1)}) custom-call(bf16[8,16,2,32,8,128]{5,4,3,2,1,0:T(8,128)(2,1)} %bitcast.7, f32[16,8192]{1,0:T(8,128)} %refs_5_.1, f32[16,8192]{1,0:T(8,128)} %refs_5_.1, ...), custom_call_target="tpu_custom_call" | custom-call | flops 8589934592 | bytes 16777216 | tf_op jit(solution)/shard_map/carried/pallas_call | solution.py:302
  25.8 4.2 %collective-permute-start = (f32[2,1024,128]{2,1,0:T(8,128)S(1)}, f32[2,1024,128]{2,1,0:T(8,128)S(1)}, u32[]{:S(2)}, u32[]{:S(2)}) collective-permute-start(f32[2,1024,128]{2,1,0:T(8,128)S(1)} %get-tuple-element.14), channel_id=1, source_target_pairs={{0,16},{16,32},{32,48},{48,64},{64,80},{80,96},{96,112},{1,17},{17... | collective-permute-start | bytes 3145736 | tf_op jit(solution)/shard_map/ppermute | solution.py:397
  30.0 24.5 %current.1 = (f32[2,1024,128]{2,1,0:T(8,128)S(1)}, bf16[2,8,16,2,8,8,128]{6,5,4,3,2,1,0:T(8,128)(2,1)S(1)}) custom-call(bf16[8,16,2,32,8,128]{5,4,3,2,1,0:T(8,128)(2,1)} %bitcast.9, f32[16,8192]{1,0:T(8,128)S(1)} %get-tuple-element.10.refs_1_, bf16[2,4096,256]{2,1,0:T(8,128)(2,1)S(1)} %get-tuple-element.11.refs_2_, ...), custom_call_target="tpu_custom_call", output_to_operand_aliasing={{1}: (3, {})} | custom-call | flops 8589934592 | bytes 16777216 | tf_op jit(solution)/shard_map/current/pallas_call | solution.py:325
  54.5 0.0 collective-permute-done.before_ref
  54.5 1.1 %messages.1 = f32[64,2,16,128]{3,2,1,0:T(8,128)S(1)} custom-call(f32[2,1024,128]{2,1,0:T(8,128)S(1)} %get-tuple-element.13.here_ref, f32[2,1024,128]{2,1,0:T(8,128)S(1)} %collective-permute-done.before_ref), custom_call_target="tpu_custom_call" | custom-call | tf_op jit(solution)/shard_map/messages/pallas_call | solution.py:271
  55.6 29.7 %all_to_all.5.got_ref = f32[128,16,128]{2,1,0:T(8,128)S(1)} all-to-all(f32[128,16,128]{2,1,0:T(8,128)S(1)} %bitcast.6), channel_id=1, replica_groups=mesh['tm'=8,'inp'=16] {'tm','inp'}, dimensions={0} | all-to-all | bytes 2097152 | tf_op jit(solution)/shard_map/all_to_all | solution.py:399
  85.3 7.5 %correlate.1 = f32[2,1,1024,1024]{3,2,1,0:T(8,128)} custom-call(f32[128,16,128]{2,1,0:T(8,128)S(1)} %all_to_all.5.got_ref), custom_call_target="tpu_custom_call" | custom-call | tf_op jit(solution)/shard_map/correlate/pallas_call | solution.py:381
Async XLA Ops:
  25.8 28.7 %collective-permute-start = (f32[2,1024,128]{2,1,0:T(8,128)S(1)}, f32[2,1024,128]{2,1,0:T(8,128)S(1)}, u32[]{:S(2)}, u32[]{:S(2)}) collective-permute-start(f32[2,1024,128]{2,1,0:T(8,128)S(1)} %get-tuple-element.14), channel_id=1, source_target_pairs={{0,16},{16,32},{32,48},{48,64},{64,80},{80,96},{96,112},{1,17},{17... | collective-permute-start | bytes 3145736 | tf_op jit(solution)/shard_map/ppermute | solution.py:397
